TPU v7x, 256 devices: a whole 4x4x8 slice. The times are simulated.
256 devices in a mesh: row: 8 (over z_hi, core), col: 32 (over y, z_lo, x).
Axes of the slice: x: 4, y: 4, z: 8 (z_hi: 4, z_lo: 2; z = z_hi * 2 + z_lo), core: 2. Of those that a mesh axis runs over, the one named last changes fastest.
Arguments:
- tokens: bfloat16 [1024, 8192], P(None, 'row'), may hold values from -50 to 50
- norm_gain: float32 [8192], P('row'), may hold values from 0.5 to 1.5
- gate_vals: bfloat16 [4096, 28672], P('row', 'col'), may hold values from -0.09375 to 0.09375
- gate_meta: int32 [2048, 28672], P('row', 'col'), may hold values from 0 to 5
- up_vals: bfloat16 [4096, 28672], P('row', 'col'), may hold values from -0.09375 to 0.09375
- up_meta: int32 [2048, 28672], P('row', 'col'), may hold values from 0 to 5
- down_vals: bfloat16 [14336, 8192], P('col', 'row'), may hold values from -0.046875 to 0.046875
- down_meta: int32 [7168, 8192], P('col', 'row'), may hold values from 0 to 5
Outputs:
- layer_out: bfloat16 [1024, 8192], P(None, 'row')
Inputs may be any that keep to these rules, and one draw needn't show every extreme that they name: `up_meta`: as for gate_meta. `down_meta`: as for gate_meta.
All inputs are finite; a program needn't handle non-finite values.
Results may differ from a plain program's by a relative error of at most 0.0075.
Values may be sent and summed in bfloat16 or wider, within the bound.
A program may use at most 128 MiB of HBM per device.

v0:
```python
import jax
import jax.numpy as jnp
from jax import lax
from jax.sharding import Mesh
from jax.sharding import PartitionSpec as P

ROW = ("row_0", "row_1")
COL = ("col_0", "col_1", "col_2")


EPS = 1e-05


def from_everyone(x, axis):
    devices = lax.axis_size(axis)
    return lax.all_to_all(jnp.broadcast_to(x[None], (devices, *x.shape)), axis, 0, 0, tiled=True)


def of_everyone(x, axis):
    return from_everyone(x, axis).sum(axis=0)


def cut_along(x, dim, devices):
    dims = x.shape
    tiles = x.reshape(*dims[:dim], devices, dims[dim] // devices, *dims[dim + 1 :])
    return jnp.moveaxis(tiles, dim, 0)


def sent_and_summed(x, axis, dim):
    devices = lax.axis_size(axis)
    tiles = lax.all_to_all(cut_along(x, dim, devices), axis, 0, 0, tiled=True)
    return jnp.sum(tiles.astype(jnp.float32), axis=0)


def summed_rows(x, axes, dim):
    far, near = axes
    tiles = cut_along(x, dim, lax.axis_size(far))
    nearer = sent_and_summed(tiles, near, dim + 1)
    arrived = lax.all_to_all(
        nearer.astype(jnp.bfloat16), far, split_axis=0, concat_axis=0, tiled=True
    )
    return arrived.astype(jnp.float32).sum(axis=0)


def in_one_piece(arrays, axis, dim, along):
    widths = [a.shape[along] for a in arrays]
    both = jnp.concatenate(arrays, axis=along)
    filled = summed_rows(both, axis, dim)
    return tuple(jnp.split(filled, [sum(widths[:k]) for k in range(1, len(widths))], axis=along))


def in_order(tiles, dim):
    tiles = jnp.moveaxis(tiles, 0, dim)
    dims = tiles.shape
    return tiles.reshape(*dims[:dim], dims[dim] * dims[dim + 1], *dims[dim + 2 :])


def whole_of(x, axes, dim):
    far, near = axes
    leading = from_everyone(x, far)
    tiles = jnp.swapaxes(from_everyone(leading, near), 0, 1)
    return in_order(tiles.reshape(-1, *x.shape), dim)


def rows_for(lines, devices):
    spare = -len(lines) % devices
    return jnp.pad(lines, [(0, spare)] + [(0, 0)] * (lines.ndim - 1))


def nested_sum(x, axes):
    lines = x.reshape(-1, x.shape[-1])
    own = summed_rows(rows_for(lines, lax.axis_size(axes[0]) * lax.axis_size(axes[1])), axes, 0)
    whole = whole_of(own.astype(jnp.bfloat16), axes, 0)
    return whole[: len(lines)].reshape(x.shape).astype(jnp.float32)


def expand(vals, meta):
    groups, cols = meta.shape
    first = jnp.where(meta < 3, 0, jnp.where(meta < 5, 1, 2))
    second = jnp.where(meta == 0, 1, jnp.where((meta == 1) | (meta == 3), 2, 3))
    pairs = vals.reshape(groups, 2, cols)
    leading = pairs[:, 0, :][:, None, :]
    trailing = pairs[:, 1, :][:, None, :]
    slots = jnp.arange(4, dtype=jnp.int32)[None, :, None]
    nothing = jnp.zeros((), vals.dtype)
    dense = jnp.where(
        first[:, None, :] == slots,
        leading,
        jnp.where(second[:, None, :] == slots, trailing, nothing),
    )
    return dense.reshape(groups * 4, cols)


def per_device(tokens, norm_gain, gate_vals, gate_meta, up_vals, up_meta, down_vals, down_meta):
    wide = tokens.astype(jnp.float32)
    squares = of_everyone(jnp.sum(wide * wide, axis=1), ROW)
    features = tokens.shape[1] * lax.axis_size(ROW)
    scale = lax.rsqrt(squares / features + EPS)
    normed = (wide * scale[:, None] * norm_gain[None, :]).astype(jnp.bfloat16)
    w_gate = expand(gate_vals, gate_meta)
    w_up = expand(up_vals, up_meta)
    gate_part = jnp.dot(normed, w_gate, preferred_element_type=jnp.float32)
    up_part = jnp.dot(normed, w_up, preferred_element_type=jnp.float32)
    gate, up_sum = in_one_piece(
        (gate_part.astype(jnp.bfloat16), up_part.astype(jnp.bfloat16)), ("row_0", "row_1"), 1, 0
    )
    portion = (jax.nn.silu(gate) * up_sum).astype(jnp.bfloat16)
    hidden = whole_of(portion, ("row_0", "row_1"), 1)
    w_down = expand(down_vals, down_meta)
    partial_down = jnp.dot(hidden, w_down, preferred_element_type=jnp.float32)
    down = nested_sum(partial_down.astype(jnp.bfloat16), ("col_0", ("col_1", "col_2")))
    return (wide + down).astype(jnp.bfloat16)


def solution(mesh):
    split = Mesh(mesh.devices.reshape(4, 2, 4, 2, 4), ("row_0", "row_1", "col_0", "col_1", "col_2"))
    return jax.shard_map(
        per_device,
        mesh=split,
        in_specs=(
            P(None, ROW),
            P(ROW),
            P(ROW, COL),
            P(ROW, COL),
            P(ROW, COL),
            P(ROW, COL),
            P(COL, ROW),
            P(COL, ROW),
        ),
        out_specs=P(None, ROW),
        check_vma=False,
    )
```

profile of v0, /device:TPU:8, one launch (start us, length us, event | category | flops | bytes accessed | tf_op | source)
XLA Modules:
  0.0 266.3 jit_solution(12274141826018444603)
XLA Ops:
  0.0 2.1 fusion
  2.8 8.5 %all-to-all-start = ((f32[8,1,1024]{2,1,0:T(1,128)}), f32[8,1,1024]{2,1,0:T(1,128)S(1)}, u32[]{:S(2)}, u32[]{:S(2)}) async-start(f32[8,1,1024]{2,1,0:T(1,128)} %broadcast_in_dim.148), calls=%async_computation | async-start | bytes 65536 | tf_op jit(solution)/shard_map/all_to_all | solution.py:16
  14.4 2.3 reshape.129
  18.0 1.5 select_select_fusion.2
  25.3 2.5 eq.151
  27.8 5.2 %eq.152 = s32[1024,896]{1,0:T(8,128)} reshape(s32[256,4,896]{2,1,0:T(4,128)} %eq.151) | data formatting | bytes 7340032 | tf_op jit(solution)/shard_map/eq | solution.py:87
  33.0 2.5 eq.160
  35.5 5.2 %eq.161 = s32[1024,896]{1,0:T(8,128)} reshape(s32[256,4,896]{2,1,0:T(4,128)} %eq.160) | data formatting | bytes 7340032 | tf_op jit(solution)/shard_map/eq | solution.py:89
  44.8 2.5 eq.163
  47.4 5.2 %eq.164 = s32[1024,896]{1,0:T(8,128)} reshape(s32[256,4,896]{2,1,0:T(4,128)} %eq.163) | data formatting | bytes 7340032 | tf_op jit(solution)/shard_map/eq | solution.py:87
  52.6 2.4 eq.169
  55.0 5.3 %eq.170 = s32[1024,896]{1,0:T(8,128)} reshape(s32[256,4,896]{2,1,0:T(4,128)} %eq.169) | data formatting | bytes 7340032 | tf_op jit(solution)/shard_map/eq | solution.py:89
  60.4 7.1 %fusion.11 = bf16[1024,896]{1,0:T(8,128)(2,1)S(1)} fusion(bf16[1024,896]{1,0:T(8,128)(2,1)} %broadcast_in_dim.154, s32[1024,896]{1,0:T(8,128)} %eq.152, bf16[1024,896]{1,0:T(8,128)(2,1)} %broadcast_in_dim.157, s32[1024,896]{1,0:T(8,128)} %eq.161, s32[1024]{0:T(1024)S(1)} %eq.154, bf16[1024,1024]{1,0:T(8,128)(2,1)S(1)} %copy-done, f32[1024]{0:T(1024)S(1)} %copy-done.17, ...), kind=kOutput, calls=%fused_computation.25 | convolution fusion | flops 1887830016 | bytes 14954496 | tf_op jit(solution)/shard_map/dot_general | solution.py:102
  67.8 2.8 %fusion.10 = bf16[1024,896]{1,0:T(8,128)(2,1)S(1)} fusion(bf16[1024,896]{1,0:T(8,128)(2,1)S(1)} %copy-done.8, s32[1024,896]{1,0:T(8,128)S(1)} %copy-done.2, bf16[1024,896]{1,0:T(8,128)(2,1)S(1)} %copy-done.9, s32[1024,896]{1,0:T(8,128)S(1)} %copy-done.3, s32[1024]{0:T(1024)S(1)} %eq.154, bf16[1024,1024]{1,0:T(8,128)(2,1)S(1)} %copy-done, ...), kind=kOutput, calls=%fused_computation.24 | convolution fusion | flops 1887830016 | bytes 14954496 | tf_op jit(solution)/shard_map/dot_general | solution.py:103
  70.6 2.1 pad_maximum_fusion
  72.7 6.1 %copy.29 = bf16[2048,896]{0,1:T(8,128)(2,1)} copy(bf16[2048,896]{1,0:T(8,128)(2,1)} %pad_maximum_fusion) | data formatting | bytes 7340032 | tf_op jit(solution)/shard_map/concatenate | solution.py:47
  78.8 2.5 copy.30
  81.3 7.7 %all_to_all.46 = bf16[2,4,2048,112]{2,3,1,0:T(8,128)(2,1)} all-to-all(bf16[2,4,2048,112]{2,3,1,0:T(8,128)(2,1)S(1)} %copy.30), channel_id=1, replica_groups=mesh['row_0'=4,'row_1'=2,'col_0'=4,'col_1'=2,'col_2'=4] {'row_1'}, dimensions={0} | all-to-all | bytes 7340032 | tf_op jit(solution)/shard_map/all_to_all | solution.py:31
  89.0 4.6 %reduce_sum.65 = bf16[4,2048,112]{1,2,0:T(8,128)(2,1)} reduce(bf16[2,4,2048,112]{2,3,1,0:T(8,128)(2,1)} %all_to_all.46, bf16[]{:T(256)} %constant.6.clone.1), dimensions={0}, to_apply=%region_2.3 | reduce | flops 917504 | bytes 5505026 | tf_op jit(solution)/shard_map/reduce_sum | solution.py:32
  93.7 7.2 %all-to-all-start.2 = ((bf16[4,2048,112]{1,2,0:T(8,128)(2,1)}), bf16[4,2048,112]{1,2,0:T(8,128)(2,1)S(1)}, u32[]{:S(2)}, u32[]{:S(2)}) async-start(bf16[4,2048,112]{1,2,0:T(8,128)(2,1)} %reduce_sum.65), calls=%async_computation.2 | async-start | bytes 3670016 | tf_op jit(solution)/shard_map/all_to_all | solution.py:39
  100.8 2.3 reshape.134
  103.2 43.2 %all-to-all-done.2 = bf16[4,2048,112]{1,2,0:T(8,128)(2,1)S(1)} async-done(((bf16[4,2048,112]{1,2,0:T(8,128)(2,1)}), bf16[4,2048,112]{1,2,0:T(8,128)(2,1)S(1)}, u32[]{:S(2)}, u32[]{:S(2)}) %all-to-all-start.2) | async-done | bytes 1835040 | tf_op jit(solution)/shard_map/all_to_all | solution.py:39
  147.8 3.7 %all-to-all-start.3 = ((bf16[4,1024,112]{1,2,0:T(8,128)(2,1)}), bf16[4,1024,112]{1,2,0:T(8,128)(2,1)S(1)}, u32[]{:S(2)}, u32[]{:S(2)}) async-start(bf16[4,1024,112]{1,2,0:T(8,128)(2,1)} %broadcast_in_dim.165), calls=%async_computation.3 | async-start | bytes 1835008 | tf_op jit(solution)/shard_map/all_to_all | solution.py:16
  154.3 4.5 %fusion.4 = bf16[224,4,1024]{2,1,0:T(4,128)(2,1)S(1)} fusion(s32[224,1024]{1,0:T(8,128)S(1)} %get-tuple-element.8, s32[224,1024]{1,0:T(8,128)S(1)} %get-tuple-element.7, bf16[224,1024]{1,0:T(8,128)(2,1)S(1)} %get-tuple-element.21, bf16[224,1024]{1,0:T(8,128)(2,1)S(1)} %get-tuple-element.22), kind=kLoop, calls=%fused_computation.11 | loop fusion | flops 3670016 | bytes 4587520 | tf_op jit(solution)/shard_map/jit(_where)/select_n | solution.py:86
  160.2 7.6 %all-to-all-done.3 = bf16[4,1024,112]{1,2,0:T(8,128)(2,1)S(1)} async-done(((bf16[4,1024,112]{1,2,0:T(8,128)(2,1)}), bf16[4,1024,112]{1,2,0:T(8,128)(2,1)S(1)}, u32[]{:S(2)}, u32[]{:S(2)}) %all-to-all-start.3) | async-done | bytes 917536 | tf_op jit(solution)/shard_map/all_to_all | solution.py:16
  168.0 5.2 %all_to_all.47 = bf16[2,4,1024,112]{2,3,1,0:T(8,128)(2,1)S(1)} all-to-all(bf16[2,4,1024,112]{2,3,1,0:T(8,128)(2,1)S(1)} %broadcast_in_dim.166), channel_id=1, replica_groups=mesh['row_0'=4,'row_1'=2,'col_0'=4,'col_1'=2,'col_2'=4] {'row_1'}, dimensions={0} | all-to-all | bytes 3670016 | tf_op jit(solution)/shard_map/all_to_all | solution.py:16
  174.7 2.4 convolution_convert_fusion
  177.4 38.7 %all_to_all.48 = bf16[8,4,32,1024]{3,2,1,0:T(8,128)(2,1)S(1)} all-to-all(bf16[8,4,32,1024]{3,2,1,0:T(8,128)(2,1)S(1)} %bitcast.37), channel_id=1, replica_groups=mesh['row_0'=4,'row_1'=2,'col_0'=4,'col_1'=2,'col_2'=4] {'col_1','col_2'}, dimensions={0} | all-to-all | bytes 4194304 | tf_op jit(solution)/shard_map/all_to_all | solution.py:31
  216.5 10.0 %all_to_all.49 = bf16[4,32,1024]{2,1,0:T(8,128)(2,1)S(1)} all-to-all(bf16[4,32,1024]{2,1,0:T(8,128)(2,1)S(1)} %reduce_sum.67), channel_id=1, replica_groups=mesh['row_0'=4,'row_1'=2,'col_0'=4,'col_1'=2,'col_2'=4] {'col_0'}, dimensions={0} | all-to-all | bytes 524288 | tf_op jit(solution)/shard_map/all_to_all | solution.py:39
  226.5 9.1 %all_to_all.50 = bf16[4,32,1024]{2,1,0:T(8,128)(2,1)S(1)} all-to-all(bf16[4,32,1024]{2,1,0:T(8,128)(2,1)S(1)} %broadcast_in_dim.175), channel_id=1, replica_groups=mesh['row_0'=4,'row_1'=2,'col_0'=4,'col_1'=2,'col_2'=4] {'col_0'}, dimensions={0} | all-to-all | bytes 524288 | tf_op jit(solution)/shard_map/all_to_all | solution.py:16
  235.9 26.7 %all_to_all.51 = bf16[8,4,32,1024]{3,2,1,0:T(8,128)(2,1)S(1)} all-to-all(bf16[8,4,32,1024]{3,2,1,0:T(8,128)(2,1)S(1)} %broadcast_in_dim.176), channel_id=1, replica_groups=mesh['row_0'=4,'row_1'=2,'col_0'=4,'col_1'=2,'col_2'=4] {'col_1','col_2'}, dimensions={0} | all-to-all | bytes 4194304 | tf_op jit(solution)/shard_map/all_to_all | solution.py:16
  264.1 2.2 fusion.3
  (71 shorter events, 25.0 us)
Async XLA Ops:
  0.0 11.2 %copy-start.13 = (bf16[512,896]{1,0:T(8,128)(2,1)S(1)}, bf16[512,896]{1,0:T(8,128)(2,1)}, u32[]{:S(2)}) copy-start(bf16[512,896]{1,0:T(8,128)(2,1)} %param.10) | copy-start | bytes 2752516
  2.8 57.5 %all-to-all-start = ((f32[8,1,1024]{2,1,0:T(1,128)}), f32[8,1,1024]{2,1,0:T(1,128)S(1)}, u32[]{:S(2)}, u32[]{:S(2)}) async-start(f32[8,1,1024]{2,1,0:T(1,128)} %broadcast_in_dim.148), calls=%async_computation | async-start | bytes 65536 | tf_op jit(solution)/shard_map/all_to_all | solution.py:16
  11.6 1.3 copy-start.14
  16.7 1.3 copy-start.15
  21.9 1.5 copy-start.12
  23.8 1.5 copy-start.7
  27.8 5.2 %copy-start.6 = (s32[256,896]{1,0:T(8,128)S(1)}, s32[256,896]{1,0:T(8,128)}, u32[]{:S(2)}) copy-start(s32[256,896]{1,0:T(8,128)} %get-tuple-element.9) | copy-start | bytes 2752516
  35.5 5.3 %copy-start.11 = (bf16[256,896]{1,0:T(8,128)(2,1)S(1)}, bf16[256,896]{1,0:T(8,128)(2,1)}, u32[]{:S(2)}) copy-start(bf16[256,896]{1,0:T(8,128)(2,1)} %get-tuple-element.18) | copy-start | bytes 1376260
  43.3 1.5 copy-start.5
  47.4 5.2 %copy-start.4 = (s32[256,896]{1,0:T(8,128)S(1)}, s32[256,896]{1,0:T(8,128)}, u32[]{:S(2)}) copy-start(s32[256,896]{1,0:T(8,128)} %get-tuple-element.13) | copy-start | bytes 2752516
  55.0 5.3 %copy-start = (bf16[1024,1024]{1,0:T(8,128)(2,1)S(1)}, bf16[1024,1024]{1,0:T(8,128)(2,1)}, u32[]{:S(2)}) copy-start(bf16[1024,1024]{1,0:T(8,128)(2,1)} %param.8) | copy-start | bytes 6291460
  55.0 5.4 %copy-start.17 = (f32[1024]{0:T(1024)S(1)}, f32[1024]{0:T(1024)}, u32[]{:S(2)}) copy-start(f32[1024]{0:T(1024)} %param.9) | copy-start | bytes 12292
  60.4 7.1 %copy-start.2 = (s32[1024,896]{1,0:T(8,128)S(1)}, s32[1024,896]{1,0:T(8,128)}, u32[]{:S(2)}) copy-start(s32[1024,896]{1,0:T(8,128)} %eq.164) | copy-start | bytes 11010052
  60.4 7.1 %copy-start.3 = (s32[1024,896]{1,0:T(8,128)S(1)}, s32[1024,896]{1,0:T(8,128)}, u32[]{:S(2)}) copy-start(s32[1024,896]{1,0:T(8,128)} %eq.170) | copy-start | bytes 11010052
  60.4 7.1 %copy-start.8 = (bf16[1024,896]{1,0:T(8,128)(2,1)S(1)}, bf16[1024,896]{1,0:T(8,128)(2,1)}, u32[]{:S(2)}) copy-start(bf16[1024,896]{1,0:T(8,128)(2,1)} %broadcast_in_dim.161) | copy-start | bytes 5505028
  60.4 7.4 %copy-start.9 = (bf16[1024,896]{1,0:T(8,128)(2,1)S(1)}, bf16[1024,896]{1,0:T(8,128)(2,1)}, u32[]{:S(2)}) copy-start(bf16[1024,896]{1,0:T(8,128)(2,1)} %broadcast_in_dim.164) | copy-start | bytes 5505028
  93.7 52.7 %all-to-all-start.2 = ((bf16[4,2048,112]{1,2,0:T(8,128)(2,1)}), bf16[4,2048,112]{1,2,0:T(8,128)(2,1)S(1)}, u32[]{:S(2)}, u32[]{:S(2)}) async-start(bf16[4,2048,112]{1,2,0:T(8,128)(2,1)} %reduce_sum.65), calls=%async_computation.2 | async-start | bytes 3670016 | tf_op jit(solution)/shard_map/all_to_all | solution.py:39
  147.8 20.0 %all-to-all-start.3 = ((bf16[4,1024,112]{1,2,0:T(8,128)(2,1)}), bf16[4,1024,112]{1,2,0:T(8,128)(2,1)S(1)}, u32[]{:S(2)}, u32[]{:S(2)}) async-start(bf16[4,1024,112]{1,2,0:T(8,128)(2,1)} %broadcast_in_dim.165), calls=%async_computation.3 | async-start | bytes 1835008 | tf_op jit(solution)/shard_map/all_to_all | solution.py:16
  152.8 1.2 copy-start.16
  173.2 1.5 copy-start.10
  262.5 1.6 copy-start.1
where the time goes:
time: 267 us; the launch traced here: 266 us
  blocking collectives  97.3 us (36%)
  local copies, waits for them, and re-layouts  66 us (25%)
  waiting for transfers between devices  50.7 us (19%)
  other arithmetic  20.2 us (8%)
  starting transfers between devices  19.4 us (7%)
  matrix products  12.3 us (5%)
    all_to_all x2, blocking collectives, sent_and_summed(): tiles = lax.all_to_all(cut_along(x, dim, devices), axis, 0, 0, tiled=True)  46.4 us
    all_to_all x1, waiting for transfers between devices, summed_rows(): lax.all_to_all(nearer.astype(jnp.bfloat16), far, split_axis=0, concat_axi...  43.2 us
    all_to_all x3, blocking collectives, from_everyone(): lax.all_to_all(jnp.broadcast_to(x[None], (devices, *x.shape)), axis, 0, 0...  41 us
    eq x6, local copies, waits for them, and re-layouts, expand(): first[:, None, :] == slots  15.6 us
    eq x4, local copies, waits for them, and re-layouts, expand(): second[:, None, :] == slots  15.5 us
    all_to_all x2, starting transfers between devices, from_everyone(): lax.all_to_all(jnp.broadcast_to(x[None], (devices, *x.shape)), axis, 0, 0...  12.2 us
    all_to_all x1, blocking collectives, summed_rows(): lax.all_to_all(nearer.astype(jnp.bfloat16), far, split_axis=0, concat_axi...  9.99 us
    all_to_all x2, waiting for transfers between devices, from_everyone(): lax.all_to_all(jnp.broadcast_to(x[None], (devices, *x.shape)), axis, 0, 0...  7.57 us
  transfers between devices with their start and end apart: 3, of which 2 were waited for; matrix products, arithmetic and copies ran while one was open for 22% of the time, Pallas kernels for 0%

commit v1 on v0

v1 whole, which is shorter than its diff:
```python
import functools

import jax
import jax.numpy as jnp
from jax import lax
from jax.experimental import pallas as pl
from jax.experimental.pallas import tpu as pltpu
from jax.sharding import PartitionSpec as P

EPS = 1e-05
MESH = pl.DeviceIdType.MESH
F32 = jnp.float32
BF16 = jnp.bfloat16

CHUNKS = 8
ROWS = 128
PIECE = 16

PAIR_IN, Z_FIRST, Z_SECOND, Z_BACK, Z_LAST, PAIR_OUT = range(6)
C_FIRST, C_SECOND, C_THIRD, G_FIRST, G_SECOND, G_THIRD = 6, 9, 12, 13, 14, 17
STAGES = 20

STEPS = ("product", "z_first", "z_second", "hidden", "z_last", "pair_out", "down", "c_second", "c_third", "g_first", "g_second", "g_third", "store")
STARTS = (0.0, 1.5, 9.0, 14.0, 18.0, 22.0, 24.0, 30.0, 33.0, 35.5, 38.0, 41.0, 46.0)
SPACING = {"product": 3.0}
PAIR_SPACING = 11.0


def step_order():
    steps = []
    for at, step in enumerate(STEPS):
        for chunk in range(CHUNKS):
            spacing = SPACING.get(step, PAIR_SPACING)
            when = STARTS[at] + (chunk // 2) * spacing + (chunk % 2) * (1.5 if step == "product" else 0.1)
            steps.append((when, at, chunk, step))
    return [(step, chunk) for _, _, chunk, step in sorted(steps)]


def planes(first, second, codes):
    none = jnp.zeros_like(first)
    yield jnp.where(codes < 3, first, none)
    yield jnp.where(codes == 0, second, jnp.where((codes == 3) | (codes == 4), first, none))
    yield jnp.where((codes == 1) | (codes == 3), second, jnp.where(codes == 5, first, none))
    yield jnp.where((codes == 2) | (codes > 3), second, none)


def one_hot(shape, of_row):
    rows = lax.broadcasted_iota(jnp.int32, shape, 0)
    columns = lax.broadcasted_iota(jnp.int32, shape, 1)
    return jnp.where(columns == of_row(rows), 1.0, 0.0).astype(BF16)


def kernel(
    tok_h, gain_h, gv_h, gm_h, uv_h, um_h, dv_h, dm_h, out_h,
    tok, gain, gv, gm, uv, um, dv, dm, wgu, wd, wp, xp,
    part, pair_in, s1, z1_in, s2, z2_in, hid, dpart, c1_in, s3, c2_in, s4, c3_in, out,
    ssq, ssq_in, scale,
    load_sem, store_sem, send, recv, ssq_send, ssq_recv,
):
    row = lax.axis_index("row")
    col = lax.axis_index("col")
    k, c = row // 2, row % 2
    y, l, x = col // 8, (col // 4) % 2, col % 4
    width = gv.shape[1]
    features = tok.shape[1]

    def on_row(k2, c2):
        return (k2 * 2 + c2, col)

    def on_col(y2, l2, x2):
        return (row, (y2 * 2 + l2) * 4 + x2)

    partner = on_row(k, 1 - c)
    beside = on_row(k + 1 - 2 * (k % 2), c)
    across = on_row(3 - k, c)

    def z_of(chunk):
        if chunk % 2 == 0:
            return beside, across, ((k + 1) // 2) % 2, k // 2
        return across, beside, k // 2, k % 2

    def first_of(chunk):
        return x if chunk % 2 == 0 else y

    def second_of(chunk):
        return y if chunk % 2 == 0 else x

    def first_peer(chunk, d):
        if chunk % 2 == 0:
            return on_col(y, l, (x + d) % 4)
        return on_col((y + d) % 4, l, x)

    def second_peer(chunk, d):
        return first_peer(chunk + 1, d)

    sources = (gv_h, gm_h, tok_h, gain_h, uv_h, um_h, dv_h, dm_h)
    places = (gv, gm, tok, gain, uv, um, dv, dm)
    loads = [pltpu.make_async_copy(a, b, load_sem.at[n]) for n, (a, b) in enumerate(zip(sources, places))]
    for load in loads:
        load.start()

    barrier = pltpu.get_barrier_semaphore()
    peers = [((row + d) % 8, col) for d in range(1, 8)]
    for d in range(1, 4):
        peers += [on_col(y, l, (x + d) % 4), on_col((y + d) % 4, l, x)]
    peers.append(on_col(y, 1 - l, x))
    for peer in peers:
        pl.semaphore_signal(barrier, inc=1, device_id=peer, device_id_type=MESH)

    split_gu = one_hot((128, 128), lambda r: jnp.where(r < 64, 2 * r, 2 * r - 127))
    split_d = one_hot((64, 64), lambda r: jnp.where(r < 32, 2 * r, 2 * r - 63))
    mix_d = one_hot((128, 128), lambda r: (r & 3) * 32 + (r >> 2))
    mix_x = one_hot((256, 256), lambda r: (r & 3) * 64 + (r >> 2))

    def expand_gu(vals, meta, offset):
        def block(b, carry):
            for j in range(width // 128):
                at = slice(j * 128, (j + 1) * 128)
                v = vals[pl.ds(pl.multiple_of(b * 128, 128), 128), at]
                both = jnp.dot(split_gu, v, preferred_element_type=F32)
                codes = meta[pl.ds(pl.multiple_of(b * 64, 64), 64), at]
                for p, plane in enumerate(planes(both[:64], both[64:], codes)):
                    wgu[pl.ds(pl.multiple_of(b * 256 + p * 64, 64), 64), offset + j * 128 : offset + (j + 1) * 128] = plane.astype(BF16)
            return carry

        lax.fori_loop(0, vals.shape[0] // 128, block, 0)

    def expand_d(b, carry):
        for j in range(wd.shape[1] // 256):
            at = slice(j * 256, (j + 1) * 256)
            v = dv[pl.ds(pl.multiple_of(b * 64, 64), 64), at]
            both = jnp.dot(split_d, v, preferred_element_type=F32)
            codes = dm[pl.ds(pl.multiple_of(b * 32, 32), 32), at]
            for p, plane in enumerate(planes(both[:32], both[32:], codes)):
                wp[p * 32 : (p + 1) * 32, :] = plane.astype(BF16)
            dense = jnp.dot(mix_d, wp[...], preferred_element_type=F32)
            wd[pl.ds(pl.multiple_of(b * 128, 128), 128), at] = dense.astype(BF16)
        return carry

    loads[0].wait()
    loads[1].wait()
    expand_gu(gv, gm, 0)
    loads[4].wait()
    loads[5].wait()
    expand_gu(uv, um, width)
    loads[2].wait()
    loads[3].wait()
    pl.semaphore_wait(barrier, len(peers))

    def copy(src, dst, chunk, stage, to):
        return pltpu.make_async_remote_copy(
            src_ref=src, dst_ref=dst, send_sem=send.at[chunk, stage], recv_sem=recv.at[chunk, stage],
            device_id=to, device_id_type=MESH,
        )

    def arrive(dst, chunk, stage):
        copy(dst, dst, chunk, stage, partner).wait_recv()

    def ssq_copy(d):
        return pltpu.make_async_remote_copy(
            src_ref=ssq, dst_ref=ssq_in.at[d - 1], send_sem=ssq_send.at[d - 1], recv_sem=ssq_recv.at[d - 1],
            device_id=((row + d) % 8, col), device_id_type=MESH,
        )

    def product(i):
        xf = tok[i * ROWS : (i + 1) * ROWS, :].astype(F32)
        sums = jnp.sum(xf * xf, axis=1, keepdims=True)
        square = (ROWS, ROWS)
        diagonal = lax.broadcasted_iota(jnp.int32, square, 0) == lax.broadcasted_iota(jnp.int32, square, 1)
        ssq[i : i + 1, :] = jnp.sum(jnp.where(diagonal, sums, 0.0), axis=0, keepdims=True)
        weighted = (xf * gain[...]).astype(BF16)
        for b in range(features // 256):
            at = slice(b * 256, (b + 1) * 256)
            xp[:, at] = jnp.dot(weighted[:, at], mix_x, preferred_element_type=F32).astype(BF16)

        def tile(n, carry):
            at = pl.ds(pl.multiple_of(n * 256, 256), 256)
            sums = jnp.dot(xp[...], wgu[:, at], preferred_element_type=F32).astype(BF16)
            part[i, :, :, :, :, at] = sums.reshape(2, 2, 2, PIECE, 256)
            return carry

        lax.fori_loop(0, wgu.shape[1] // 256, tile, 0)
        copy(part.at[i, 1 - c], pair_in.at[i], i, PAIR_IN, partner).start()
        if i == CHUNKS - 1:
            for d in range(1, 8):
                ssq_copy(d).start()

    def z_first(i):
        p1, _, h, u = z_of(i)
        arrive(pair_in.at[i], i, PAIR_IN)
        s1[i] = (part[i, c, 1 - h].astype(F32) + pair_in[i, 1 - h].astype(F32)).astype(BF16)
        copy(s1.at[i], z1_in.at[i], i, Z_FIRST, p1).start()

    def held(i, h, u):
        return part[i, c, h, u].astype(F32) + pair_in[i, h, u].astype(F32) + z1_in[i, u].astype(F32)

    def z_second(i):
        _, p2, h, u = z_of(i)
        arrive(z1_in.at[i], i, Z_FIRST)
        s2[i] = held(i, h, 1 - u).astype(BF16)
        copy(s2.at[i], z2_in.at[i], i, Z_SECOND, p2).start()

    def hidden(i):
        _, p2, h, u = z_of(i)
        if i == 0:
            total = ssq[...]
            for d in range(1, 8):
                ssq_copy(d).wait_recv()
                total = total + ssq_in[d - 1]
            scale[...] = lax.rsqrt(total / (features * 8) + EPS)
        lanes = (PIECE, ROWS)
        mine = c * 64 + (2 * h + u) * PIECE + lax.broadcasted_iota(jnp.int32, lanes, 0)
        chosen = lax.broadcasted_iota(jnp.int32, lanes, 1) == mine
        factor = jnp.sum(jnp.where(chosen, scale[i : i + 1, :], 0.0), axis=1, keepdims=True)
        arrive(z2_in.at[i], i, Z_SECOND)
        sums = (held(i, h, u) + z2_in[i].astype(F32)) * factor
        gate, up = sums[:, :width], sums[:, width:]
        hid[i, c, h, u] = (gate / (1.0 + jnp.exp(-gate)) * up).astype(BF16)
        copy(hid.at[i, c, h, u], hid.at[i, c, h, u], i, Z_BACK, p2).start()

    def z_last(i):
        p1, _, h, u = z_of(i)
        arrive(hid.at[i, c, h, 1 - u], i, Z_BACK)
        copy(hid.at[i, c, h], hid.at[i, c, h], i, Z_LAST, p1).start()

    def pair_out(i):
        _, _, h, _ = z_of(i)
        arrive(hid.at[i, c, 1 - h], i, Z_LAST)
        copy(hid.at[i, c], hid.at[i, c], i, PAIR_OUT, partner).start()

    def down(i):
        if i == 0:
            loads[6].wait()
            loads[7].wait()
            lax.fori_loop(0, dv.shape[0] // 64, expand_d, 0)
        arrive(hid.at[i, 1 - c], i, PAIR_OUT)

        def tile(n, carry):
            at = pl.ds(pl.multiple_of(n * 256, 256), 256)
            sums = jnp.dot(hid[i].reshape(ROWS, width), wd[:, at], preferred_element_type=F32).astype(BF16)
            dpart[i, :, :, at] = sums.reshape(4, 32, 256)
            return carry

        lax.fori_loop(0, wd.shape[1] // 256, tile, 0)
        a = first_of(i)
        for d in range(1, 4):
            copy(dpart.at[i, (a + d) % 4], c1_in.at[i, d - 1], i, C_FIRST + d - 1, first_peer(i, d)).start()

    def c_second(i):
        a, b = first_of(i), second_of(i)
        total = dpart[i, a].astype(F32)
        for d in range(1, 4):
            arrive(c1_in.at[i, d - 1], i, C_FIRST + d - 1)
            total = total + c1_in[i, d - 1].astype(F32)
        total = total.astype(BF16)
        for q in range(4):
            s3[i, q] = total[:, q * 256 : (q + 1) * 256]
        for d in range(1, 4):
            copy(s3.at[i, (b + d) % 4], c2_in.at[i, d - 1], i, C_SECOND + d - 1, second_peer(i, d)).start()

    def c_third(i):
        total = s3[i, second_of(i)].astype(F32)
        for d in range(1, 4):
            arrive(c2_in.at[i, d - 1], i, C_SECOND + d - 1)
            total = total + c2_in[i, d - 1].astype(F32)
        total = total.astype(BF16)
        for q in range(2):
            s4[i, q] = total[:, q * 128 : (q + 1) * 128]
        copy(s4.at[i, 1 - l], c3_in.at[i], i, C_THIRD, on_col(y, 1 - l, x)).start()

    def columns_of(i, place):
        return pl.ds(pl.multiple_of(second_of(i) * 256 + place * 128, 128), 128)

    def g_first(i):
        a = first_of(i)
        at = columns_of(i, l)
        arrive(c3_in.at[i], i, C_THIRD)
        own = tok[pl.ds(pl.multiple_of(i * ROWS + a * 32, 32), 32), at].astype(F32)
        out[i, a, :, at] = (own + s4[i, l].astype(F32) + c3_in[i].astype(F32)).astype(BF16)
        copy(out.at[i, a, :, at], out.at[i, a, :, at], i, G_FIRST, on_col(y, 1 - l, x)).start()

    def block_of(i, b):
        return out.at[i, first_of(i), :, pl.ds(pl.multiple_of(b * 256, 256), 256)]

    def g_second(i):
        arrive(out.at[i, first_of(i), :, columns_of(i, 1 - l)], i, G_FIRST)
        mine = block_of(i, second_of(i))
        for d in range(1, 4):
            copy(mine, mine, i, G_SECOND + d - 1, second_peer(i, d)).start()

    def g_third(i):
        a, b = first_of(i), second_of(i)
        for d in range(1, 4):
            arrive(block_of(i, (b + 4 - d) % 4), i, G_SECOND + d - 1)
        for d in range(1, 4):
            copy(out.at[i, a], out.at[i, a], i, G_THIRD + d - 1, first_peer(i, d)).start()

    def stored(i):
        return pltpu.make_async_copy(out.at[i], out_h.at[i], store_sem.at[i])

    def store(i):
        a = first_of(i)
        for d in range(1, 4):
            arrive(out.at[i, (a + 4 - d) % 4], i, G_THIRD + d - 1)
        stored(i).start()

    bodies = dict(
        product=product, z_first=z_first, z_second=z_second, hidden=hidden, z_last=z_last, pair_out=pair_out, down=down,
        c_second=c_second, c_third=c_third, g_first=g_first, g_second=g_second, g_third=g_third, store=store,
    )
    for step, chunk in step_order():
        bodies[step](chunk)

    def sent(src, chunk, stage):
        copy(src, src, chunk, stage, partner).wait_send()

    def finish(i, carry):
        sent(pair_in.at[i], i, PAIR_IN)
        sent(s1.at[i], i, Z_FIRST)
        sent(s2.at[i], i, Z_SECOND)
        sent(hid.at[i, 0, 0, 0], i, Z_BACK)
        sent(hid.at[i, 0, 0], i, Z_LAST)
        sent(hid.at[i, 0], i, PAIR_OUT)
        sent(c3_in.at[i], i, C_THIRD)
        sent(c3_in.at[i], i, G_FIRST)
        for d in range(3):
            sent(c1_in.at[i, d], i, C_FIRST + d)
            sent(c2_in.at[i, d], i, C_SECOND + d)
            sent(c2_in.at[i, d], i, G_SECOND + d)
            sent(c1_in.at[i, d], i, G_THIRD + d)
        stored(i).wait()
        return carry

    lax.fori_loop(0, CHUNKS, finish, 0)
    for d in range(1, 8):
        ssq_copy(d).wait_send()


def per_device(tokens, norm_gain, gate_vals, gate_meta, up_vals, up_meta, down_vals, down_meta):
    batch, features = tokens.shape
    width = gate_vals.shape[1]
    pieces = (2, 2, PIECE)
    vmem = pltpu.VMEM
    scratch = [
        vmem(tokens.shape, BF16), vmem((1, features), F32),
        vmem(gate_vals.shape, BF16), vmem(gate_meta.shape, jnp.int32),
        vmem(up_vals.shape, BF16), vmem(up_meta.shape, jnp.int32),
        vmem(down_vals.shape, BF16), vmem(down_meta.shape, jnp.int32),
        vmem((features, 2 * width), BF16), vmem((width, features), BF16), vmem((128, 256), BF16), vmem((ROWS, features), BF16),
        vmem((CHUNKS, 2, *pieces, 2 * width), BF16), vmem((CHUNKS, *pieces, 2 * width), BF16),
        vmem((CHUNKS, 2, PIECE, 2 * width), BF16), vmem((CHUNKS, 2, PIECE, 2 * width), BF16),
        vmem((CHUNKS, PIECE, 2 * width), BF16), vmem((CHUNKS, PIECE, 2 * width), BF16),
        vmem((CHUNKS, 2, *pieces, width), BF16),
        vmem((CHUNKS, 4, 32, features), BF16), vmem((CHUNKS, 3, 32, features), BF16),
        vmem((CHUNKS, 4, 32, 256), BF16), vmem((CHUNKS, 3, 32, 256), BF16),
        vmem((CHUNKS, 2, 32, 128), BF16), vmem((CHUNKS, 32, 128), BF16),
        vmem((CHUNKS, 4, 32, features), BF16),
        vmem((CHUNKS, ROWS), F32), vmem((7, CHUNKS, ROWS), F32), vmem((CHUNKS, ROWS), F32),
        pltpu.SemaphoreType.DMA((8,)), pltpu.SemaphoreType.DMA((CHUNKS,)),
        pltpu.SemaphoreType.DMA((CHUNKS, STAGES)), pltpu.SemaphoreType.DMA((CHUNKS, STAGES)),
        pltpu.SemaphoreType.DMA((7,)), pltpu.SemaphoreType.DMA((7,)),
    ]
    anywhere = pl.BlockSpec(memory_space=pl.ANY)
    out = pl.pallas_call(
        kernel,
        out_shape=jax.ShapeDtypeStruct((CHUNKS, 4, 32, features), BF16),
        in_specs=[anywhere] * 8,
        out_specs=anywhere,
        scratch_shapes=scratch,
        compiler_params=pltpu.CompilerParams(collective_id=0, has_side_effects=True, vmem_limit_bytes=60 * 1024 * 1024),
    )(tokens, norm_gain.reshape(1, features), gate_vals, gate_meta, up_vals, up_meta, down_vals, down_meta)
    return out.reshape(batch, features)


def solution(mesh):
    return jax.shard_map(
        per_device,
        mesh=mesh,
        in_specs=(
            P(None, "row"),
            P("row"),
            P("row", "col"),
            P("row", "col"),
            P("row", "col"),
            P("row", "col"),
            P("col", "row"),
            P("col", "row"),
        ),
        out_specs=P(None, "row"),
        check_vma=False,
    )
```

time: 267 us -> 123 us (0.46)
  Pallas kernels: 0 us -> 119 us
  blocking collectives: 97.3 us -> 0 us
  local copies, waits for them, and re-layouts: 66 us -> 3.08 us
  waiting for transfers between devices: 50.7 us -> 0 us
  other arithmetic: 20.2 us -> 0 us
  starting transfers between devices: 19.4 us -> 0 us
  matrix products: 12.3 us -> 0 us
    pallas_call x0 -> x1, Pallas kernels: none -> 119 us  [per_device(): pl.pallas_call(kernel, out_shape=jax.ShapeDtypeStruct((CHUNKS, 4, 32, fea...]
    all_to_all x6 -> x0, blocking collectives: 97.3 us -> none  [the longest x2 46.4 us: sent_and_summed(): tiles = lax.all_to_all(cut_along(x, dim, devices), axis, 0, 0, tiled=True)]
    all_to_all x3 -> x0, waiting for transfers between devices: 50.7 us -> none  [the longest x1 43.2 us: summed_rows(): lax.all_to_all(nearer.astype(jnp.bfloat16), far, split_axis=0, concat_axi...]
    eq x10 -> x0, local copies, waits for them, and re-layouts: 31 us -> none  [the longest x6 15.6 us: expand(): first[:, None, :] == slots]
    all_to_all x3 -> x0, starting transfers between devices: 19.4 us -> none  [the longest x2 12.2 us: from_everyone(): lax.all_to_all(jnp.broadcast_to(x[None], (devices, *x.shape)), axis, 0, 0...]
    dot_general x3 -> x0, matrix products: 12.3 us -> none  [the longest x1 7.08 us: per_device(): gate_part = jnp.dot(normed, w_gate, preferred_element_type=jnp.float32)]
    broadcast_in_dim x13 -> x0, local copies, waits for them, and re-layouts: 9.96 us -> none  [the longest x4 3.94 us: expand(): jnp.where(second[:, None, :] == slots, trailing, nothing)]
    select_n x4 -> x0, other arithmetic: 7.78 us -> none  [the longest x1 4.46 us: expand(): jnp.where(first[:, None, :] == slots, leading, jnp.where(second[:, None,...]
  transfers between devices with their start and end apart: 3 -> 0, of which waited for: 2 -> 0; matrix products, arithmetic and copies ran while one was open for 22% -> 0% of each run, Pallas kernels for 0% -> 0%
where the time goes in v1:
time: 123 us; the launch traced here: 122 us
  Pallas kernels  119 us (97%)
  local copies, waits for them, and re-layouts  3.08 us (3%)
    pallas_call x1, Pallas kernels, per_device(): pl.pallas_call(kernel, out_shape=jax.ShapeDtypeStruct((CHUNKS, 4, 32, fea...  119 us
    unnamed x1, local copies, waits for them, and re-layouts  3.08 us

profile of v1, /device:TPU:8, one launch (start us, length us, event | category | flops | bytes accessed | tf_op | source)
XLA Modules:
  0.0 121.9 jit_solution(14766022925006534595)
XLA Ops:
  0.0 118.8 %shard_map.82 = bf16[8,4,32,1024]{3,2,1,0:T(8,128)(2,1)} custom-call(bf16[1024,1024]{1,0:T(8,128)(2,1)} %tok_h.1, f32[1,1024]{1,0:T(1,128)} %bitcast.3, bf16[512,896]{1,0:T(8,128)(2,1)} %gv_h.1, s32[256,896]{1,0:T(8,128)} %gm_h.1, bf16[512,896]{1,0:T(8,128)(2,1)} %uv_h.1, s32[256,896]{1,0:T(8,128)} %um_h.1, bf16[448,1024]{1,0:T(8,128)(2,1)} %dv_h.1, ...), custom_call_target="tpu_custom_call" | custom-call | tf_op jit(solution)/shard_map/pallas_call | solution.py:364
  118.8 3.1 %copy.10 = bf16[1024,1024]{1,0:T(8,128)(2,1)} copy(bf16[1024,1024]{1,0:T(8,128)(2,1)} %bitcast.2) | data formatting | bytes 4194304

commit v2 on v1

--- a/solution.py
+++ b/solution.py
@@ -16,24 +16,24 @@
 ROWS = 128
 PIECE = 16
 
-PAIR_IN, Z_FIRST, Z_SECOND, Z_BACK, Z_LAST, PAIR_OUT = range(6)
-C_FIRST, C_SECOND, C_THIRD, G_FIRST, G_SECOND, G_THIRD = 6, 9, 12, 13, 14, 17
-STAGES = 20
-
-STEPS = ("product", "z_first", "z_second", "hidden", "z_last", "pair_out", "down", "c_second", "c_third", "g_first", "g_second", "g_third", "store")
-STARTS = (0.0, 1.5, 9.0, 14.0, 18.0, 22.0, 24.0, 30.0, 33.0, 35.5, 38.0, 41.0, 46.0)
-SPACING = {"product": 3.0}
-PAIR_SPACING = 11.0
+PAIR_IN, Z_FIRST, Z_SECOND, Z_BACK, Z_LAST, PAIR_OUT, BETWEEN = range(7)
+F_OUT, S_OUT, S_BACK, F_BACK = 7, 10, 13, 16
+STAGES = 19
+
+STEPS = (
+    "squares", "expand_down", "product", "z_first", "z_second", "hidden", "z_last", "pair_out", "down", "s_out", "between", "s_back",
+    "f_back", "store",
+)
+ORDER = (
+    16, 0, 24, 25, 22, 18, 20, 26, 31, 32, 27, 29, 28, 33, 30, 40, 34, 8, 36, 41, 35, 39, 37, 49,
+    42, 43, 38, 48, 44, 45, 57, 50, 51, 56, 65, 47, 46, 64, 52, 53, 58, 59, 66, 55, 67, 54, 60, 73,
+    61, 72, 68, 69, 62, 63, 75, 74, 80, 70, 81, 76, 71, 77, 88, 89, 83, 82, 84, 85, 91, 78, 90, 79,
+    92, 97, 96, 86, 99, 93, 87, 100, 104, 94, 95, 105, 98, 101, 107, 102, 108, 103, 109, 106, 111, 110,
+)
 
 
 def step_order():
-    steps = []
-    for at, step in enumerate(STEPS):
-        for chunk in range(CHUNKS):
-            spacing = SPACING.get(step, PAIR_SPACING)
-            when = STARTS[at] + (chunk // 2) * spacing + (chunk % 2) * (1.5 if step == "product" else 0.1)
-            steps.append((when, at, chunk, step))
-    return [(step, chunk) for _, _, chunk, step in sorted(steps)]
+    return [(STEPS[n // CHUNKS], n % CHUNKS) for n in ORDER]
 
 
 def planes(first, second, codes):
@@ -53,7 +53,7 @@
 def kernel(
     tok_h, gain_h, gv_h, gm_h, uv_h, um_h, dv_h, dm_h, out_h,
     tok, gain, gv, gm, uv, um, dv, dm, wgu, wd, wp, xp,
-    part, pair_in, s1, z1_in, s2, z2_in, hid, dpart, c1_in, s3, c2_in, s4, c3_in, out,
+    part, pair_in, s1, z1_in, s2, z2_in, hid, dpart, f_in, s4, s_in, s5, t_in, out,
     ssq, ssq_in, scale,
     load_sem, store_sem, send, recv, ssq_send, ssq_recv,
 ):
@@ -71,13 +71,15 @@
         return (row, (y2 * 2 + l2) * 4 + x2)
 
     partner = on_row(k, 1 - c)
-    beside = on_row(k + 1 - 2 * (k % 2), c)
-    across = on_row(3 - k, c)
+
+    def ways(n, way):
+        if way == 0:
+            return n + 1 - 2 * (n % 2), 3 - n, ((n + 1) // 2) % 2, n // 2
+        return 3 - n, n + 1 - 2 * (n % 2), n // 2, n % 2
 
     def z_of(chunk):
-        if chunk % 2 == 0:
-            return beside, across, ((k + 1) // 2) % 2, k // 2
-        return across, beside, k // 2, k % 2
+        p1, p2, h, u = ways(k, chunk % 2)
+        return on_row(p1, c), on_row(p2, c), h, u
 
     def first_of(chunk):
         return x if chunk % 2 == 0 else y
@@ -92,6 +94,8 @@
 
     def second_peer(chunk, d):
         return first_peer(chunk + 1, d)
+
+    opposite = on_col(y, 1 - l, x)
 
     sources = (gv_h, gm_h, tok_h, gain_h, uv_h, um_h, dv_h, dm_h)
     places = (gv, gm, tok, gain, uv, um, dv, dm)
@@ -145,7 +149,6 @@
     expand_gu(uv, um, width)
     loads[2].wait()
     loads[3].wait()
-    pl.semaphore_wait(barrier, len(peers))
 
     def copy(src, dst, chunk, stage, to):
         return pltpu.make_async_remote_copy(
@@ -162,28 +165,34 @@
             device_id=((row + d) % 8, col), device_id_type=MESH,
         )
 
+    def squares(i):
+        def rows(n, carry):
+            xf = tok[pl.ds(pl.multiple_of(n * ROWS, ROWS), ROWS), :].astype(F32)
+            sums = jnp.sum(xf * xf, axis=1, keepdims=True)
+            square = (ROWS, ROWS)
+            diagonal = lax.broadcasted_iota(jnp.int32, square, 0) == lax.broadcasted_iota(jnp.int32, square, 1)
+            ssq[pl.ds(n, 1), :] = jnp.sum(jnp.where(diagonal, sums, 0.0), axis=0, keepdims=True)
+            return carry
+
+        lax.fori_loop(0, CHUNKS, rows, 0)
+        for d in range(1, 8):
+            ssq_copy(d).start()
+
+    first_chunk = min(ORDER, key=lambda n: n // CHUNKS != 2) % CHUNKS
+
     def product(i):
-        xf = tok[i * ROWS : (i + 1) * ROWS, :].astype(F32)
-        sums = jnp.sum(xf * xf, axis=1, keepdims=True)
-        square = (ROWS, ROWS)
-        diagonal = lax.broadcasted_iota(jnp.int32, square, 0) == lax.broadcasted_iota(jnp.int32, square, 1)
-        ssq[i : i + 1, :] = jnp.sum(jnp.where(diagonal, sums, 0.0), axis=0, keepdims=True)
-        weighted = (xf * gain[...]).astype(BF16)
+        weighted = (tok[i * ROWS : (i + 2) * ROWS, :].astype(F32) * gain[...]).astype(BF16)
         for b in range(features // 256):
             at = slice(b * 256, (b + 1) * 256)
             xp[:, at] = jnp.dot(weighted[:, at], mix_x, preferred_element_type=F32).astype(BF16)
-
-        def tile(n, carry):
-            at = pl.ds(pl.multiple_of(n * 256, 256), 256)
+        for n in range(2 * width // 256):
+            at = slice(n * 256, (n + 1) * 256)
             sums = jnp.dot(xp[...], wgu[:, at], preferred_element_type=F32).astype(BF16)
-            part[i, :, :, :, :, at] = sums.reshape(2, 2, 2, PIECE, 256)
-            return carry
-
-        lax.fori_loop(0, wgu.shape[1] // 256, tile, 0)
-        copy(part.at[i, 1 - c], pair_in.at[i], i, PAIR_IN, partner).start()
-        if i == CHUNKS - 1:
-            for d in range(1, 8):
-                ssq_copy(d).start()
+            part[i : i + 2, :, :, :, :, at] = sums.reshape(2, 2, 2, 2, PIECE, 256)
+        if i == first_chunk:
+            pl.semaphore_wait(barrier, len(peers))
+        for j in (i, i + 1):
+            copy(part.at[j, 1 - c], pair_in.at[j], j, PAIR_IN, partner).start()
 
     def z_first(i):
         p1, _, h, u = z_of(i)
@@ -228,72 +237,59 @@
         arrive(hid.at[i, c, 1 - h], i, Z_LAST)
         copy(hid.at[i, c], hid.at[i, c], i, PAIR_OUT, partner).start()
 
+    def expand_down(i):
+        loads[6].wait()
+        loads[7].wait()
+        lax.fori_loop(0, dv.shape[0] // 64, expand_d, 0)
+
     def down(i):
-        if i == 0:
-            loads[6].wait()
-            loads[7].wait()
-            lax.fori_loop(0, dv.shape[0] // 64, expand_d, 0)
         arrive(hid.at[i, 1 - c], i, PAIR_OUT)
-
-        def tile(n, carry):
-            at = pl.ds(pl.multiple_of(n * 256, 256), 256)
+        for n in range(wd.shape[1] // 256):
+            at = slice(n * 256, (n + 1) * 256)
             sums = jnp.dot(hid[i].reshape(ROWS, width), wd[:, at], preferred_element_type=F32).astype(BF16)
             dpart[i, :, :, at] = sums.reshape(4, 32, 256)
-            return carry
-
-        lax.fori_loop(0, wd.shape[1] // 256, tile, 0)
         a = first_of(i)
         for d in range(1, 4):
-            copy(dpart.at[i, (a + d) % 4], c1_in.at[i, d - 1], i, C_FIRST + d - 1, first_peer(i, d)).start()
-
-    def c_second(i):
+            copy(dpart.at[i, (a + d) % 4], f_in.at[i, d - 1], i, F_OUT + d - 1, first_peer(i, d)).start()
+
+    def s_out(i):
         a, b = first_of(i), second_of(i)
         total = dpart[i, a].astype(F32)
         for d in range(1, 4):
-            arrive(c1_in.at[i, d - 1], i, C_FIRST + d - 1)
-            total = total + c1_in[i, d - 1].astype(F32)
+            arrive(f_in.at[i, d - 1], i, F_OUT + d - 1)
+            total = total + f_in[i, d - 1].astype(F32)
         total = total.astype(BF16)
         for q in range(4):
-            s3[i, q] = total[:, q * 256 : (q + 1) * 256]
-        for d in range(1, 4):
-            copy(s3.at[i, (b + d) % 4], c2_in.at[i, d - 1], i, C_SECOND + d - 1, second_peer(i, d)).start()
-
-    def c_third(i):
-        total = s3[i, second_of(i)].astype(F32)
-        for d in range(1, 4):
-            arrive(c2_in.at[i, d - 1], i, C_SECOND + d - 1)
-            total = total + c2_in[i, d - 1].astype(F32)
-        total = total.astype(BF16)
-        for q in range(2):
-            s4[i, q] = total[:, q * 128 : (q + 1) * 128]
-        copy(s4.at[i, 1 - l], c3_in.at[i], i, C_THIRD, on_col(y, 1 - l, x)).start()
-
-    def columns_of(i, place):
-        return pl.ds(pl.multiple_of(second_of(i) * 256 + place * 128, 128), 128)
-
-    def g_first(i):
-        a = first_of(i)
-        at = columns_of(i, l)
-        arrive(c3_in.at[i], i, C_THIRD)
-        own = tok[pl.ds(pl.multiple_of(i * ROWS + a * 32, 32), 32), at].astype(F32)
-        out[i, a, :, at] = (own + s4[i, l].astype(F32) + c3_in[i].astype(F32)).astype(BF16)
-        copy(out.at[i, a, :, at], out.at[i, a, :, at], i, G_FIRST, on_col(y, 1 - l, x)).start()
-
-    def block_of(i, b):
-        return out.at[i, first_of(i), :, pl.ds(pl.multiple_of(b * 256, 256), 256)]
-
-    def g_second(i):
-        arrive(out.at[i, first_of(i), :, columns_of(i, 1 - l)], i, G_FIRST)
-        mine = block_of(i, second_of(i))
-        for d in range(1, 4):
-            copy(mine, mine, i, G_SECOND + d - 1, second_peer(i, d)).start()
-
-    def g_third(i):
+            s4[i, q] = total[:, q * 256 : (q + 1) * 256]
+        for d in range(1, 4):
+            copy(s4.at[i, (b + d) % 4], s_in.at[i, d - 1], i, S_OUT + d - 1, second_peer(i, d)).start()
+
+    def between(i):
+        total = s4[i, second_of(i)].astype(F32)
+        for d in range(1, 4):
+            arrive(s_in.at[i, d - 1], i, S_OUT + d - 1)
+            total = total + s_in[i, d - 1].astype(F32)
+        s5[i] = total.astype(BF16)
+        copy(s5.at[i], t_in.at[i], i, BETWEEN, opposite).start()
+
+    def columns_of(b):
+        return pl.ds(pl.multiple_of(b * 256, 256), 256)
+
+    def s_back(i):
         a, b = first_of(i), second_of(i)
-        for d in range(1, 4):
-            arrive(block_of(i, (b + 4 - d) % 4), i, G_SECOND + d - 1)
-        for d in range(1, 4):
-            copy(out.at[i, a], out.at[i, a], i, G_THIRD + d - 1, first_peer(i, d)).start()
+        own = tok[pl.ds(pl.multiple_of(i * ROWS + a * 32, 32), 32), columns_of(b)].astype(F32)
+        arrive(t_in.at[i], i, BETWEEN)
+        out[i, a, :, columns_of(b)] = (own + (s5[i].astype(F32) + t_in[i].astype(F32))).astype(BF16)
+        mine = out.at[i, a, :, columns_of(b)]
+        for d in range(1, 4):
+            copy(mine, mine, i, S_BACK + d - 1, second_peer(i, d)).start()
+
+    def f_back(i):
+        a, b = first_of(i), second_of(i)
+        for d in range(1, 4):
+            arrive(out.at[i, a, :, columns_of((b + 4 - d) % 4)], i, S_BACK + d - 1)
+        for d in range(1, 4):
+            copy(out.at[i, a], out.at[i, a], i, F_BACK + d - 1, first_peer(i, d)).start()
 
     def stored(i):
         return pltpu.make_async_copy(out.at[i], out_h.at[i], store_sem.at[i])
@@ -301,14 +297,15 @@
     def store(i):
         a = first_of(i)
         for d in range(1, 4):
-            arrive(out.at[i, (a + 4 - d) % 4], i, G_THIRD + d - 1)
+            arrive(out.at[i, (a + 4 - d) % 4], i, F_BACK + d - 1)
         stored(i).start()
 
     bodies = dict(
-        product=product, z_first=z_first, z_second=z_second, hidden=hidden, z_last=z_last, pair_out=pair_out, down=down,
-        c_second=c_second, c_third=c_third, g_first=g_first, g_second=g_second, g_third=g_third, store=store,
+        squares=squares, product=product, z_first=z_first, z_second=z_second, hidden=hidden, z_last=z_last, pair_out=pair_out,
+        expand_down=expand_down, down=down, s_out=s_out, between=between, s_back=s_back, f_back=f_back, store=store,
     )
-    for step, chunk in step_order():
+    order = step_order()
+    for step, chunk in order:
         bodies[step](chunk)
 
     def sent(src, chunk, stage):
@@ -321,13 +318,12 @@
         sent(hid.at[i, 0, 0, 0], i, Z_BACK)
         sent(hid.at[i, 0, 0], i, Z_LAST)
         sent(hid.at[i, 0], i, PAIR_OUT)
-        sent(c3_in.at[i], i, C_THIRD)
-        sent(c3_in.at[i], i, G_FIRST)
+        sent(t_in.at[i], i, BETWEEN)
         for d in range(3):
-            sent(c1_in.at[i, d], i, C_FIRST + d)
-            sent(c2_in.at[i, d], i, C_SECOND + d)
-            sent(c2_in.at[i, d], i, G_SECOND + d)
-            sent(c1_in.at[i, d], i, G_THIRD + d)
+            sent(f_in.at[i, d], i, F_OUT + d)
+            sent(s_in.at[i, d], i, S_OUT + d)
+            sent(s_in.at[i, d], i, S_BACK + d)
+            sent(f_in.at[i, d], i, F_BACK + d)
         stored(i).wait()
         return carry
 
@@ -346,14 +342,14 @@
         vmem(gate_vals.shape, BF16), vmem(gate_meta.shape, jnp.int32),
         vmem(up_vals.shape, BF16), vmem(up_meta.shape, jnp.int32),
         vmem(down_vals.shape, BF16), vmem(down_meta.shape, jnp.int32),
-        vmem((features, 2 * width), BF16), vmem((width, features), BF16), vmem((128, 256), BF16), vmem((ROWS, features), BF16),
+        vmem((features, 2 * width), BF16), vmem((width, features), BF16), vmem((128, 256), BF16), vmem((2 * ROWS, features), BF16),
         vmem((CHUNKS, 2, *pieces, 2 * width), BF16), vmem((CHUNKS, *pieces, 2 * width), BF16),
         vmem((CHUNKS, 2, PIECE, 2 * width), BF16), vmem((CHUNKS, 2, PIECE, 2 * width), BF16),
         vmem((CHUNKS, PIECE, 2 * width), BF16), vmem((CHUNKS, PIECE, 2 * width), BF16),
         vmem((CHUNKS, 2, *pieces, width), BF16),
         vmem((CHUNKS, 4, 32, features), BF16), vmem((CHUNKS, 3, 32, features), BF16),
         vmem((CHUNKS, 4, 32, 256), BF16), vmem((CHUNKS, 3, 32, 256), BF16),
-        vmem((CHUNKS, 2, 32, 128), BF16), vmem((CHUNKS, 32, 128), BF16),
+        vmem((CHUNKS, 32, 256), BF16), vmem((CHUNKS, 32, 256), BF16),
         vmem((CHUNKS, 4, 32, features), BF16),
         vmem((CHUNKS, ROWS), F32), vmem((7, CHUNKS, ROWS), F32), vmem((CHUNKS, ROWS), F32),
         pltpu.SemaphoreType.DMA((8,)), pltpu.SemaphoreType.DMA((CHUNKS,)),

time: 123 us -> 94.6 us (0.77)
  Pallas kernels: 119 us -> 90.8 us
    pallas_call x1, Pallas kernels: 119 us -> 90.8 us  [per_device(): pl.pallas_call(kernel, out_shape=jax.ShapeDtypeStruct((CHUNKS, 4, 32, fea...]
where the time goes in v2:
time: 94.6 us; the launch traced here: 93.9 us
  Pallas kernels  90.8 us (96%)
  local copies, waits for them, and re-layouts  3.08 us (3%)
    pallas_call x1, Pallas kernels, per_device(): pl.pallas_call(kernel, out_shape=jax.ShapeDtypeStruct((CHUNKS, 4, 32, fea...  90.8 us
    unnamed x1, local copies, waits for them, and re-layouts  3.08 us

profile of v2, /device:TPU:8, one launch (start us, length us, event | category | flops | bytes accessed | tf_op | source)
XLA Modules:
  0.0 93.9 jit_solution(5487654224243551892)
XLA Ops:
  0.0 90.8 %shard_map.82 = bf16[8,4,32,1024]{3,2,1,0:T(8,128)(2,1)} custom-call(bf16[1024,1024]{1,0:T(8,128)(2,1)} %tok_h.1, f32[1,1024]{1,0:T(1,128)} %bitcast.3, bf16[512,896]{1,0:T(8,128)(2,1)} %gv_h.1, s32[256,896]{1,0:T(8,128)} %gm_h.1, bf16[512,896]{1,0:T(8,128)(2,1)} %uv_h.1, s32[256,896]{1,0:T(8,128)} %um_h.1, bf16[448,1024]{1,0:T(8,128)(2,1)} %dv_h.1, ...), custom_call_target="tpu_custom_call" | custom-call | tf_op jit(solution)/shard_map/pallas_call | solution.py:360
  90.8 3.1 %copy.10 = bf16[1024,1024]{1,0:T(8,128)(2,1)} copy(bf16[1024,1024]{1,0:T(8,128)(2,1)} %bitcast.2) | data formatting | bytes 4194304

commit v3 on v2

v3 whole, which is shorter than its diff:
```python
import functools

import jax
import jax.numpy as jnp
from jax import lax
from jax.experimental import pallas as pl
from jax.experimental.pallas import tpu as pltpu
from jax.sharding import PartitionSpec as P

EPS = 1e-05
MESH = pl.DeviceIdType.MESH
F32 = jnp.float32
BF16 = jnp.bfloat16

CHUNKS = 8
ROWS = 128
PIECE = 16

PAIR_IN, Z_FIRST, Z_SECOND, Z_BACK, Z_LAST, PAIR_OUT, F_OUT, S_OUT, BETWEEN, S_BACK, F_BACK = range(11)
STAGES = 11

STEPS = (
    "squares", "expand_down", "product", "z_first", "z_second", "hidden", "z_last", "pair_out", "down", "s_out", "between", "s_back",
    "f_back", "arrive",
)
ORDER = (
    18, 0, 26, 27, 16, 25, 20, 34, 24, 29, 22, 42, 33, 30, 8, 32, 50, 41, 28, 35, 38, 58, 31, 49,
    40, 37, 43, 46, 36, 66, 39, 48, 57, 45, 74, 65, 54, 51, 44, 47, 56, 53, 64, 62, 59, 82, 73, 70,
    52, 67, 55, 61, 72, 81, 69, 78, 90, 60, 75, 89, 63, 68, 80, 77, 71, 86, 83, 98, 76, 85, 94, 88,
    91, 79, 97, 84, 93, 106, 102, 99, 87, 92, 105, 96, 95, 101, 110, 100, 107, 104, 103, 109, 108, 111,
)


def step_order():
    return [(STEPS[n // CHUNKS], n % CHUNKS) for n in ORDER]


def planes(first, second, codes):
    none = jnp.zeros_like(first)
    yield jnp.where(codes < 3, first, none)
    yield jnp.where(codes == 0, second, jnp.where((codes == 3) | (codes == 4), first, none))
    yield jnp.where((codes == 1) | (codes == 3), second, jnp.where(codes == 5, first, none))
    yield jnp.where((codes == 2) | (codes > 3), second, none)


def one_hot(shape, of_row):
    rows = lax.broadcasted_iota(jnp.int32, shape, 0)
    columns = lax.broadcasted_iota(jnp.int32, shape, 1)
    return jnp.where(columns == of_row(rows), 1.0, 0.0).astype(BF16)


def kernel(
    tok_h, gain_h, gv_h, gm_h, uv_h, um_h, dv_h, dm_h, out,
    tok, gain, gv, gm, uv, um, dv, dm, wgu, wd, wp, xp,
    part, pair_in, s1, z1_in, s2, z2_in, hid, dpart, f_in, s4, s_in, s5, t_in,
    ssq, ssq_in, scale,
    load_sem, send, recv, ssq_sem,
):
    row = lax.axis_index("row")
    col = lax.axis_index("col")
    k, c = row // 2, row % 2
    y, l, x = col // 8, (col // 4) % 2, col % 4
    width = gv.shape[1]
    features = tok.shape[1]

    def on_row(k2, c2):
        return (k2 * 2 + c2, col)

    def on_col(y2, l2, x2):
        return (row, (y2 * 2 + l2) * 4 + x2)

    partner = on_row(k, 1 - c)

    def ways(n, way):
        near, far = n + 1 - 2 * (n % 2), 3 - n
        return (near, far) if way == 0 else (far, near)

    def z_of(way):
        p1, p2 = ways(k, way)
        return p1, p2, ways(p1, way)[1]

    def to_z(n):
        return on_row(n, c)

    def first_of(v):
        return x if v == 0 else y

    def second_of(v):
        return y if v == 0 else x

    def first_peer(v, d):
        if v == 0:
            return on_col(y, l, (x + d) % 4)
        return on_col((y + d) % 4, l, x)

    def second_peer(v, d):
        return first_peer(1 - v, d)

    opposite = on_col(y, 1 - l, x)

    sources = (gv_h, gm_h, tok_h, gain_h, uv_h, um_h, dv_h, dm_h)
    places = (gv, gm, tok, gain, uv, um, dv, dm)
    loads = [pltpu.make_async_copy(a, b, load_sem.at[n]) for n, (a, b) in enumerate(zip(sources, places))]
    for load in loads:
        load.start()

    barrier = pltpu.get_barrier_semaphore()
    peers = [((row + d) % 8, col) for d in range(1, 8)]
    for d in range(1, 4):
        peers += [on_col(y, l, (x + d) % 4), on_col((y + d) % 4, l, x)]
    peers.append(on_col(y, 1 - l, x))
    for peer in peers:
        pl.semaphore_signal(barrier, inc=1, device_id=peer, device_id_type=MESH)

    split_gu = one_hot((128, 128), lambda r: jnp.where(r < 64, 2 * r, 2 * r - 127))
    split_d = one_hot((64, 64), lambda r: jnp.where(r < 32, 2 * r, 2 * r - 63))
    mix_d = one_hot((128, 128), lambda r: (r & 3) * 32 + (r >> 2))
    mix_x = one_hot((256, 256), lambda r: (r & 3) * 64 + (r >> 2))

    def expand_gu(vals, meta, offset):
        def block(b, carry):
            for j in range(width // 128):
                at = slice(j * 128, (j + 1) * 128)
                v = vals[pl.ds(pl.multiple_of(b * 128, 128), 128), at]
                both = jnp.dot(split_gu, v, preferred_element_type=F32)
                codes = meta[pl.ds(pl.multiple_of(b * 64, 64), 64), at]
                for p, plane in enumerate(planes(both[:64], both[64:], codes)):
                    wgu[pl.ds(pl.multiple_of(b * 256 + p * 64, 64), 64), offset + j * 128 : offset + (j + 1) * 128] = plane.astype(BF16)
            return carry

        lax.fori_loop(0, vals.shape[0] // 128, block, 0)

    def expand_d(b, carry):
        for j in range(wd.shape[1] // 256):
            at = slice(j * 256, (j + 1) * 256)
            v = dv[pl.ds(pl.multiple_of(b * 64, 64), 64), at]
            both = jnp.dot(split_d, v, preferred_element_type=F32)
            codes = dm[pl.ds(pl.multiple_of(b * 32, 32), 32), at]
            for p, plane in enumerate(planes(both[:32], both[32:], codes)):
                wp[p * 32 : (p + 1) * 32, :] = plane.astype(BF16)
            dense = jnp.dot(mix_d, wp[...], preferred_element_type=F32)
            wd[pl.ds(pl.multiple_of(b * 128, 128), 128), at] = dense.astype(BF16)
        return carry

    loads[0].wait()
    loads[1].wait()
    expand_gu(gv, gm, 0)
    loads[4].wait()
    loads[5].wait()
    expand_gu(uv, um, width)
    loads[2].wait()
    loads[3].wait()

    def copy(src, dst, chunk, stage, to):
        return pltpu.make_async_remote_copy(
            src_ref=src, dst_ref=dst, send_sem=send.at[stage], recv_sem=recv.at[chunk, stage],
            device_id=to, device_id_type=MESH,
        )

    def arrive(dst, chunk, stage):
        copy(dst, dst, chunk, stage, partner).wait_recv()

    def ssq_copy(d):
        return pltpu.make_async_remote_copy(
            src_ref=ssq, dst_ref=ssq_in.at[d - 1], send_sem=ssq_sem.at[0], recv_sem=ssq_sem.at[1],
            device_id=((row + d) % 8, col), device_id_type=MESH,
        )

    def all_squares():
        return pltpu.make_async_remote_copy(
            src_ref=ssq_in, dst_ref=ssq_in, send_sem=ssq_sem.at[0], recv_sem=ssq_sem.at[1],
            device_id=partner, device_id_type=MESH,
        )

    def squares(i):
        def rows(n, carry):
            xf = tok[pl.ds(pl.multiple_of(n * ROWS, ROWS), ROWS), :].astype(F32)
            sums = jnp.sum(xf * xf, axis=1, keepdims=True)
            square = (ROWS, ROWS)
            diagonal = lax.broadcasted_iota(jnp.int32, square, 0) == lax.broadcasted_iota(jnp.int32, square, 1)
            ssq[pl.ds(n, 1), :] = jnp.sum(jnp.where(diagonal, sums, 0.0), axis=0, keepdims=True)
            return carry

        lax.fori_loop(0, CHUNKS, rows, 0)
        for d in range(1, 8):
            ssq_copy(d).start()

    order = step_order()
    first_chunk = [chunk for step, chunk in order if step == "product"][0]
    first_hidden = [chunk for step, chunk in order if step == "hidden"][0]

    def product(i):
        weighted = (tok[i * ROWS : (i + 2) * ROWS, :].astype(F32) * gain[...]).astype(BF16)
        for b in range(features // 256):
            at = slice(b * 256, (b + 1) * 256)
            xp[:, at] = jnp.dot(weighted[:, at], mix_x, preferred_element_type=F32).astype(BF16)
        for n in range(2 * width // 256):
            at = slice(n * 256, (n + 1) * 256)
            sums = jnp.dot(xp[...], wgu[:, at], preferred_element_type=F32).astype(BF16)
            part[i : i + 2, :, :, :, at] = sums.reshape(2, 2, 4, PIECE, 256)
        if i == first_chunk:
            pl.semaphore_wait(barrier, len(peers))
        for j in (i, i + 1):
            copy(part.at[j, 1 - c], pair_in.at[j], j, PAIR_IN, partner).start()

    def sums_of(w):
        return slice(w * width, (w + 1) * width)

    def paired(i, n, w):
        return part[i, c, n, :, sums_of(w)].astype(F32) + pair_in[i, n, :, sums_of(w)].astype(F32)

    def z_first(i):
        arrive(pair_in.at[i], i, PAIR_IN)
        for w in range(2):
            p1, _, other = z_of(w)
            s1[i, w, 0] = paired(i, p1, w).astype(BF16)
            s1[i, w, 1] = paired(i, other, w).astype(BF16)
            copy(s1.at[i, w], z1_in.at[i, w], i, Z_FIRST, to_z(p1)).start()

    def z_second(i):
        arrive(z1_in.at[i], i, Z_FIRST)
        for w in range(2):
            _, p2, _ = z_of(w)
            s2[i, w] = (paired(i, p2, w) + z1_in[i, w, 1].astype(F32)).astype(BF16)
            copy(s2.at[i, w], z2_in.at[i, w], i, Z_SECOND, to_z(p2)).start()

    def part_of(i, n, w):
        return hid.at[i, c, n, :, slice(0, 512) if w == 0 else slice(512, width)]

    def hidden(i):
        if i == first_hidden:
            all_squares().wait_recv()
            total = ssq[...]
            for d in range(1, 8):
                total = total + ssq_in[d - 1]
            scale[...] = lax.rsqrt(total / (features * 8) + EPS)
        lanes = (PIECE, ROWS)
        mine = c * 64 + k * PIECE + lax.broadcasted_iota(jnp.int32, lanes, 0)
        chosen = lax.broadcasted_iota(jnp.int32, lanes, 1) == mine
        factor = jnp.sum(jnp.where(chosen, scale[i : i + 1, :], 0.0), axis=1, keepdims=True)
        both = []
        arrive(z2_in.at[i], i, Z_SECOND)
        for w in range(2):
            both.append((paired(i, k, w) + z1_in[i, w, 0].astype(F32) + z2_in[i, w].astype(F32)) * factor)
        gate, up = both
        hid[i, c, k] = (gate / (1.0 + jnp.exp(-gate)) * up).astype(BF16)
        for w in range(2):
            mine = part_of(i, k, w)
            copy(mine, mine, i, Z_BACK, to_z(z_of(w)[1])).start()

    def z_last(i):
        arrive(hid.at[i, c, 0], i, Z_BACK)
        for w in range(2):
            p1, p2, _ = z_of(w)
            for mine in (part_of(i, k, w), part_of(i, p2, w)):
                copy(mine, mine, i, Z_LAST, to_z(p1)).start()

    def pair_out(i):
        arrive(hid.at[i, c, 0:2], i, Z_LAST)
        copy(hid.at[i, c], hid.at[i, c], i, PAIR_OUT, partner).start()

    def expand_down(i):
        loads[6].wait()
        loads[7].wait()
        lax.fori_loop(0, dv.shape[0] // 64, expand_d, 0)

    def down(i):
        arrive(hid.at[i, 1 - c], i, PAIR_OUT)
        for n in range(wd.shape[1] // 256):
            at = slice(n * 256, (n + 1) * 256)
            sums = jnp.dot(hid[i].reshape(ROWS, width), wd[:, at], preferred_element_type=F32).astype(BF16)
            dpart[i, :, :, :, at] = sums.reshape(2, 4, PIECE, 256)
        for v in range(2):
            for d in range(1, 4):
                src = dpart.at[i, v, (first_of(v) + d) % 4]
                copy(src, f_in.at[i, v, d - 1], i, F_OUT, first_peer(v, d)).start()

    def s_out(i):
        arrive(f_in.at[i], i, F_OUT)
        for v in range(2):
            total = dpart[i, v, first_of(v)].astype(F32)
            for d in range(1, 4):
                total = total + f_in[i, v, d - 1].astype(F32)
            total = total.astype(BF16)
            for q in range(4):
                s4[i, v, q] = total[:, q * 256 : (q + 1) * 256]
            for d in range(1, 4):
                src = s4.at[i, v, (second_of(v) + d) % 4]
                copy(src, s_in.at[i, v, d - 1], i, S_OUT, second_peer(v, d)).start()

    def between(i):
        arrive(s_in.at[i], i, S_OUT)
        for v in range(2):
            total = s4[i, v, second_of(v)].astype(F32)
            for d in range(1, 4):
                total = total + s_in[i, v, d - 1].astype(F32)
            s5[i, v] = total.astype(BF16)
        copy(s5.at[i], t_in.at[i], i, BETWEEN, opposite).start()

    def block_of(i, v, b):
        return out.at[i, v, first_of(v), :, pl.ds(pl.multiple_of(b * 256, 256), 256)]

    def s_back(i):
        arrive(t_in.at[i], i, BETWEEN)
        for v in range(2):
            rows = pl.ds(pl.multiple_of(i * ROWS + v * 64 + first_of(v) * PIECE, PIECE), PIECE)
            columns = pl.ds(pl.multiple_of(second_of(v) * 256, 256), 256)
            own = tok[rows, columns].astype(F32)
            result = own + (s5[i, v].astype(F32) + t_in[i, v].astype(F32))
            out[i, v, first_of(v), :, columns] = result.astype(BF16)
            mine = block_of(i, v, second_of(v))
            for d in range(1, 4):
                copy(mine, mine, i, S_BACK, second_peer(v, d)).start()

    def f_back(i):
        arrive(s_in.at[i], i, S_BACK)
        for v in range(2):
            mine = out.at[i, v, first_of(v)]
            for d in range(1, 4):
                copy(mine, mine, i, F_BACK, first_peer(v, d)).start()

    def arrived(i):
        arrive(f_in.at[i], i, F_BACK)

    bodies = dict(
        squares=squares, product=product, z_first=z_first, z_second=z_second, hidden=hidden, z_last=z_last, pair_out=pair_out,
        expand_down=expand_down, down=down, s_out=s_out, between=between, s_back=s_back, f_back=f_back, arrive=arrived,
    )
    for step, chunk in order:
        bodies[step](chunk)

    for stage, whole in (
        (PAIR_IN, pair_in), (Z_FIRST, z1_in), (Z_SECOND, z2_in), (Z_BACK, hid.at[:, 0, 0]), (Z_LAST, hid.at[:, 0, 0:2]),
        (PAIR_OUT, hid.at[:, 0]), (F_OUT, f_in), (S_OUT, s_in), (BETWEEN, t_in), (S_BACK, s_in), (F_BACK, f_in),
    ):
        copy(whole, whole, 0, stage, partner).wait_send()
    all_squares().wait_send()


def per_device(tokens, norm_gain, gate_vals, gate_meta, up_vals, up_meta, down_vals, down_meta):
    batch, features = tokens.shape
    width = gate_vals.shape[1]
    vmem = pltpu.VMEM
    scratch = [
        vmem(tokens.shape, BF16), vmem((1, features), F32),
        vmem(gate_vals.shape, BF16), vmem(gate_meta.shape, jnp.int32),
        vmem(up_vals.shape, BF16), vmem(up_meta.shape, jnp.int32),
        vmem(down_vals.shape, BF16), vmem(down_meta.shape, jnp.int32),
        vmem((features, 2 * width), BF16), vmem((width, features), BF16), vmem((128, 256), BF16), vmem((2 * ROWS, features), BF16),
        vmem((CHUNKS, 2, 4, PIECE, 2 * width), BF16), vmem((CHUNKS, 4, PIECE, 2 * width), BF16),
        vmem((CHUNKS, 2, 2, PIECE, width), BF16), vmem((CHUNKS, 2, 2, PIECE, width), BF16),
        vmem((CHUNKS, 2, PIECE, width), BF16), vmem((CHUNKS, 2, PIECE, width), BF16),
        vmem((CHUNKS, 2, 4, PIECE, width), BF16),
        vmem((CHUNKS, 2, 4, PIECE, features), BF16), vmem((CHUNKS, 2, 3, PIECE, features), BF16),
        vmem((CHUNKS, 2, 4, PIECE, 256), BF16), vmem((CHUNKS, 2, 3, PIECE, 256), BF16),
        vmem((CHUNKS, 2, PIECE, 256), BF16), vmem((CHUNKS, 2, PIECE, 256), BF16),
        vmem((CHUNKS, ROWS), F32), vmem((7, CHUNKS, ROWS), F32), vmem((CHUNKS, ROWS), F32),
        pltpu.SemaphoreType.DMA((8,)),
        pltpu.SemaphoreType.DMA((STAGES,)), pltpu.SemaphoreType.DMA((CHUNKS, STAGES)), pltpu.SemaphoreType.DMA((2,)),
    ]
    anywhere = pl.BlockSpec(memory_space=pl.ANY)
    out = pl.pallas_call(
        kernel,
        out_shape=pltpu.VMEM((CHUNKS, 2, 4, PIECE, features), BF16),
        in_specs=[anywhere] * 8,
        out_specs=pl.BlockSpec(memory_space=pltpu.VMEM),
        scratch_shapes=scratch,
        compiler_params=pltpu.CompilerParams(collective_id=0, has_side_effects=True, vmem_limit_bytes=60 * 1024 * 1024),
    )(tokens, norm_gain.reshape(1, features), gate_vals, gate_meta, up_vals, up_meta, down_vals, down_meta)
    return out.reshape(batch, features)


def solution(mesh):
    return jax.shard_map(
        per_device,
        mesh=mesh,
        in_specs=(
            P(None, "row"),
            P("row"),
            P("row", "col"),
            P("row", "col"),
            P("row", "col"),
            P("row", "col"),
            P("col", "row"),
            P("col", "row"),
        ),
        out_specs=P(None, "row"),
        check_vma=False,
    )
```

time: 94.6 us -> 87.5 us (0.925)
  Pallas kernels: 90.8 us -> 86 us
  local copies, waits for them, and re-layouts: 3.08 us -> 1.32 us
    pallas_call x1, Pallas kernels: 90.8 us -> 86 us  [per_device(): pl.pallas_call(kernel, out_shape=pltpu.VMEM((CHUNKS, 2, 4, PIECE, feature...]
    unnamed x1, local copies, waits for them, and re-layouts: 3.08 us -> 1.32 us
where the time goes in v3:
time: 87.5 us; the launch traced here: 87.3 us
  Pallas kernels  86 us (98%)
  local copies, waits for them, and re-layouts  1.32 us (2%)
    pallas_call x1, Pallas kernels, per_device(): pl.pallas_call(kernel, out_shape=pltpu.VMEM((CHUNKS, 2, 4, PIECE, feature...  86 us

profile of v3, /device:TPU:8, one launch (start us, length us, event | category | flops | bytes accessed | tf_op | source)
XLA Modules:
  0.0 87.3 jit_solution(7797916420776830031)
XLA Ops:
  0.0 86.0 %shard_map.82 = bf16[8,2,4,16,1024]{4,3,2,1,0:T(8,128)(2,1)S(1)} custom-call(bf16[1024,1024]{1,0:T(8,128)(2,1)} %tok_h.1, f32[1,1024]{1,0:T(1,128)} %bitcast.3, bf16[512,896]{1,0:T(8,128)(2,1)} %gv_h.1, s32[256,896]{1,0:T(8,128)} %gm_h.1, bf16[512,896]{1,0:T(8,128)(2,1)} %uv_h.1, s32[256,896]{1,0:T(8,128)} %um_h.1, bf16[448,1024]{1,0:T(8,128)(2,1)} %dv_h.1, ...), custom_call_target="tpu_custom_call" | custom-call | tf_op jit(solution)/shard_map/pallas_call | solution.py:362
  86.0 1.3 %copy.10 = bf16[1024,1024]{1,0:T(8,128)(2,1)} copy(bf16[1024,1024]{1,0:T(8,128)(2,1)S(1)} %bitcast.2) | data formatting | bytes 4194304

commit v4 on v3

--- a/solution.py
+++ b/solution.py
@@ -24,10 +24,10 @@
     "f_back", "arrive",
 )
 ORDER = (
-    18, 0, 26, 27, 16, 25, 20, 34, 24, 29, 22, 42, 33, 30, 8, 32, 50, 41, 28, 35, 38, 58, 31, 49,
-    40, 37, 43, 46, 36, 66, 39, 48, 57, 45, 74, 65, 54, 51, 44, 47, 56, 53, 64, 62, 59, 82, 73, 70,
-    52, 67, 55, 61, 72, 81, 69, 78, 90, 60, 75, 89, 63, 68, 80, 77, 71, 86, 83, 98, 76, 85, 94, 88,
-    91, 79, 97, 84, 93, 106, 102, 99, 87, 92, 105, 96, 95, 101, 110, 100, 107, 104, 103, 109, 108, 111,
+    16, 24, 25, 22, 20, 30, 0, 32, 31, 18, 38, 27, 40, 39, 46, 28, 48, 47, 54, 26, 56, 35, 55, 33,
+    62, 29, 8, 70, 34, 63, 43, 36, 64, 71, 41, 37, 78, 42, 51, 44, 49, 72, 79, 45, 50, 86, 59, 52,
+    57, 67, 53, 58, 65, 60, 87, 94, 80, 66, 75, 61, 68, 73, 69, 95, 88, 74, 83, 102, 81, 76, 91, 77,
+    103, 82, 89, 96, 110, 84, 90, 99, 85, 92, 111, 97, 93, 104, 98, 107, 100, 101, 105, 106, 108, 109,
 )
 
 
@@ -35,10 +35,12 @@
     return [(STEPS[n // CHUNKS], n % CHUNKS) for n in ORDER]
 
 
-def planes(first, second, codes):
+def planes(first, second, meta):
+    codes = meta.astype(F32).astype(BF16)
     none = jnp.zeros_like(first)
-    yield jnp.where(codes < 3, first, none)
-    yield jnp.where(codes == 0, second, jnp.where((codes == 3) | (codes == 4), first, none))
+    low = codes < 3
+    yield jnp.where(low, first, none)
+    yield jnp.where(low, jnp.where(codes == 0, second, none), jnp.where(codes < 5, first, none))
     yield jnp.where((codes == 1) | (codes == 3), second, jnp.where(codes == 5, first, none))
     yield jnp.where((codes == 2) | (codes > 3), second, none)
 
@@ -54,7 +56,7 @@
     tok, gain, gv, gm, uv, um, dv, dm, wgu, wd, wp, xp,
     part, pair_in, s1, z1_in, s2, z2_in, hid, dpart, f_in, s4, s_in, s5, t_in,
     ssq, ssq_in, scale,
-    load_sem, send, recv, ssq_sem,
+    load_sem, block_sem, send, recv, ssq_sem,
 ):
     row = lax.axis_index("row")
     col = lax.axis_index("col")
@@ -98,9 +100,19 @@
 
     opposite = on_col(y, 1 - l, x)
 
-    sources = (gv_h, gm_h, tok_h, gain_h, uv_h, um_h, dv_h, dm_h)
-    places = (gv, gm, tok, gain, uv, um, dv, dm)
+    def block_load(src, dst, n, b):
+        rows = src.shape[0] // 4
+        at = pl.ds(pl.multiple_of(b * rows, rows), rows)
+        return pltpu.make_async_copy(src.at[at], dst.at[at], block_sem.at[n, b])
+
+    blocks = ((gv_h, gv), (gm_h, gm), (uv_h, uv), (um_h, um))
+    sources = (tok_h, gain_h, dv_h, dm_h)
+    places = (tok, gain, dv, dm)
     loads = [pltpu.make_async_copy(a, b, load_sem.at[n]) for n, (a, b) in enumerate(zip(sources, places))]
+    for n in range(2):
+        for b in range(4):
+            block_load(*blocks[2 * n], 2 * n, b).start()
+            block_load(*blocks[2 * n + 1], 2 * n + 1, b).start()
     for load in loads:
         load.start()
 
@@ -117,39 +129,37 @@
     mix_d = one_hot((128, 128), lambda r: (r & 3) * 32 + (r >> 2))
     mix_x = one_hot((256, 256), lambda r: (r & 3) * 64 + (r >> 2))
 
-    def expand_gu(vals, meta, offset):
+    def expand_gu(vals, meta, offset, n):
         def block(b, carry):
+            block_load(*blocks[n], n, b).wait()
+            block_load(*blocks[n + 1], n + 1, b).wait()
             for j in range(width // 128):
                 at = slice(j * 128, (j + 1) * 128)
                 v = vals[pl.ds(pl.multiple_of(b * 128, 128), 128), at]
-                both = jnp.dot(split_gu, v, preferred_element_type=F32)
+                both = jnp.dot(split_gu, v, preferred_element_type=F32).astype(BF16)
                 codes = meta[pl.ds(pl.multiple_of(b * 64, 64), 64), at]
                 for p, plane in enumerate(planes(both[:64], both[64:], codes)):
-                    wgu[pl.ds(pl.multiple_of(b * 256 + p * 64, 64), 64), offset + j * 128 : offset + (j + 1) * 128] = plane.astype(BF16)
+                    wgu[pl.ds(pl.multiple_of(b * 256 + p * 64, 64), 64), offset + j * 128 : offset + (j + 1) * 128] = plane
             return carry
 
-        lax.fori_loop(0, vals.shape[0] // 128, block, 0)
+        lax.fori_loop(0, 4, block, 0, unroll=True)
 
     def expand_d(b, carry):
         for j in range(wd.shape[1] // 256):
             at = slice(j * 256, (j + 1) * 256)
             v = dv[pl.ds(pl.multiple_of(b * 64, 64), 64), at]
-            both = jnp.dot(split_d, v, preferred_element_type=F32)
+            both = jnp.dot(split_d, v, preferred_element_type=F32).astype(BF16)
             codes = dm[pl.ds(pl.multiple_of(b * 32, 32), 32), at]
             for p, plane in enumerate(planes(both[:32], both[32:], codes)):
-                wp[p * 32 : (p + 1) * 32, :] = plane.astype(BF16)
+                wp[p * 32 : (p + 1) * 32, :] = plane
             dense = jnp.dot(mix_d, wp[...], preferred_element_type=F32)
             wd[pl.ds(pl.multiple_of(b * 128, 128), 128), at] = dense.astype(BF16)
         return carry
 
+    expand_gu(gv, gm, 0, 0)
+    expand_gu(uv, um, width, 2)
     loads[0].wait()
     loads[1].wait()
-    expand_gu(gv, gm, 0)
-    loads[4].wait()
-    loads[5].wait()
-    expand_gu(uv, um, width)
-    loads[2].wait()
-    loads[3].wait()
 
     def copy(src, dst, chunk, stage, to):
         return pltpu.make_async_remote_copy(
@@ -189,19 +199,30 @@
     first_chunk = [chunk for step, chunk in order if step == "product"][0]
     first_hidden = [chunk for step, chunk in order if step == "hidden"][0]
 
-    def product(i):
-        weighted = (tok[i * ROWS : (i + 2) * ROWS, :].astype(F32) * gain[...]).astype(BF16)
+    def multiply(i, count):
+        rows = slice(0, count * ROWS)
+        weighted = (tok[i * ROWS : (i + count) * ROWS, :].astype(F32) * gain[...]).astype(BF16)
         for b in range(features // 256):
             at = slice(b * 256, (b + 1) * 256)
-            xp[:, at] = jnp.dot(weighted[:, at], mix_x, preferred_element_type=F32).astype(BF16)
+            xp[rows, at] = jnp.dot(weighted[:, at], mix_x, preferred_element_type=F32).astype(BF16)
         for n in range(2 * width // 256):
             at = slice(n * 256, (n + 1) * 256)
-            sums = jnp.dot(xp[...], wgu[:, at], preferred_element_type=F32).astype(BF16)
-            part[i : i + 2, :, :, :, at] = sums.reshape(2, 2, 4, PIECE, 256)
+            sums = jnp.dot(xp[rows, :], wgu[:, at], preferred_element_type=F32).astype(BF16)
+            part[i : i + count, :, :, :, at] = sums.reshape(count, 2, 4, PIECE, 256)
+
+    def to_partner(i):
+        copy(part.at[i, 1 - c], pair_in.at[i], i, PAIR_IN, partner).start()
+
+    def product(i):
         if i == first_chunk:
+            multiply(i, 1)
             pl.semaphore_wait(barrier, len(peers))
-        for j in (i, i + 1):
-            copy(part.at[j, 1 - c], pair_in.at[j], j, PAIR_IN, partner).start()
+            to_partner(i)
+            multiply(i + 1, 1)
+        else:
+            multiply(i, 2)
+            to_partner(i)
+        to_partner(i + 1)
 
     def sums_of(w):
         return slice(w * width, (w + 1) * width)
@@ -260,9 +281,9 @@
         copy(hid.at[i, c], hid.at[i, c], i, PAIR_OUT, partner).start()
 
     def expand_down(i):
-        loads[6].wait()
-        loads[7].wait()
-        lax.fori_loop(0, dv.shape[0] // 64, expand_d, 0)
+        loads[2].wait()
+        loads[3].wait()
+        lax.fori_loop(0, dv.shape[0] // 64, expand_d, 0, unroll=True)
 
     def down(i):
         arrive(hid.at[i, 1 - c], i, PAIR_OUT)
@@ -355,7 +376,7 @@
         vmem((CHUNKS, 2, 4, PIECE, 256), BF16), vmem((CHUNKS, 2, 3, PIECE, 256), BF16),
         vmem((CHUNKS, 2, PIECE, 256), BF16), vmem((CHUNKS, 2, PIECE, 256), BF16),
         vmem((CHUNKS, ROWS), F32), vmem((7, CHUNKS, ROWS), F32), vmem((CHUNKS, ROWS), F32),
-        pltpu.SemaphoreType.DMA((8,)),
+        pltpu.SemaphoreType.DMA((4,)), pltpu.SemaphoreType.DMA((4, 4)),
         pltpu.SemaphoreType.DMA((STAGES,)), pltpu.SemaphoreType.DMA((CHUNKS, STAGES)), pltpu.SemaphoreType.DMA((2,)),
     ]
     anywhere = pl.BlockSpec(memory_space=pl.ANY)

time: 87.5 us -> 86 us (0.983)
  Pallas kernels: 86 us -> 83.8 us
    pallas_call x1, Pallas kernels: 86 us -> 83.8 us  [per_device(): pl.pallas_call(kernel, out_shape=pltpu.VMEM((CHUNKS, 2, 4, PIECE, feature...]
where the time goes in v4:
time: 86 us; the launch traced here: 85.1 us
  Pallas kernels  83.8 us (97%)
  local copies, waits for them, and re-layouts  1.32 us (2%)
    pallas_call x1, Pallas kernels, per_device(): pl.pallas_call(kernel, out_shape=pltpu.VMEM((CHUNKS, 2, 4, PIECE, feature...  83.8 us

profile of v4, /device:TPU:8, one launch (start us, length us, event | category | flops | bytes accessed | tf_op | source)
XLA Modules:
  0.0 85.1 jit_solution(2537480414943633153)
XLA Ops:
  0.0 83.8 %shard_map.82 = bf16[8,2,4,16,1024]{4,3,2,1,0:T(8,128)(2,1)S(1)} custom-call(bf16[1024,1024]{1,0:T(8,128)(2,1)} %tok_h.1, f32[1,1024]{1,0:T(1,128)} %bitcast.3, bf16[512,896]{1,0:T(8,128)(2,1)} %gv_h.1, s32[256,896]{1,0:T(8,128)} %gm_h.1, bf16[512,896]{1,0:T(8,128)(2,1)} %uv_h.1, s32[256,896]{1,0:T(8,128)} %um_h.1, bf16[448,1024]{1,0:T(8,128)(2,1)} %dv_h.1, ...), custom_call_target="tpu_custom_call" | custom-call | tf_op jit(solution)/shard_map/pallas_call | solution.py:383
  83.8 1.3 %copy.10 = bf16[1024,1024]{1,0:T(8,128)(2,1)} copy(bf16[1024,1024]{1,0:T(8,128)(2,1)S(1)} %bitcast.2) | data formatting | bytes 4194304

commit v5 on v4

--- a/solution.py
+++ b/solution.py
@@ -16,18 +16,20 @@
 ROWS = 128
 PIECE = 16
 
-PAIR_IN, Z_FIRST, Z_SECOND, Z_BACK, Z_LAST, PAIR_OUT, F_OUT, S_OUT, BETWEEN, S_BACK, F_BACK = range(11)
-STAGES = 11
+PAIR_IN, Z_FIRST, Z_SECOND, Z_BACK, Z_LAST, PAIR_OUT, F_OUT, S_OUT, BETWEEN, S_BACK, F_BACK, PAIR_GATE, PAIR_UP = range(13)
+STAGES = 13
 
 STEPS = (
     "squares", "expand_down", "product", "z_first", "z_second", "hidden", "z_last", "pair_out", "down", "s_out", "between", "s_back",
     "f_back", "arrive",
 )
+FAR_FIRST = (2, 1, 3)
+
 ORDER = (
-    16, 24, 25, 22, 20, 30, 0, 32, 31, 18, 38, 27, 40, 39, 46, 28, 48, 47, 54, 26, 56, 35, 55, 33,
-    62, 29, 8, 70, 34, 63, 43, 36, 64, 71, 41, 37, 78, 42, 51, 44, 49, 72, 79, 45, 50, 86, 59, 52,
-    57, 67, 53, 58, 65, 60, 87, 94, 80, 66, 75, 61, 68, 73, 69, 95, 88, 74, 83, 102, 81, 76, 91, 77,
-    103, 82, 89, 96, 110, 84, 90, 99, 85, 92, 111, 97, 93, 104, 98, 107, 100, 101, 105, 106, 108, 109,
+    16, 24, 20, 25, 22, 29, 0, 32, 33, 31, 18, 37, 41, 40, 27, 39, 49, 48, 45, 26, 35, 57, 30, 47,
+    56, 28, 34, 53, 8, 65, 38, 64, 43, 36, 42, 55, 61, 73, 46, 51, 69, 44, 50, 81, 63, 72, 54, 71,
+    59, 52, 77, 58, 89, 67, 62, 66, 80, 79, 60, 70, 85, 68, 75, 93, 74, 87, 88, 78, 97, 76, 83, 95,
+    101, 82, 86, 91, 96, 105, 84, 90, 94, 103, 109, 92, 99, 104, 98, 102, 111, 100, 107, 106, 110, 108,
 )
 
 
@@ -113,8 +115,8 @@
         for b in range(4):
             block_load(*blocks[2 * n], 2 * n, b).start()
             block_load(*blocks[2 * n + 1], 2 * n + 1, b).start()
-    for load in loads:
-        load.start()
+        loads[2 * n].start()
+        loads[2 * n + 1].start()
 
     barrier = pltpu.get_barrier_semaphore()
     peers = [((row + d) % 8, col) for d in range(1, 8)]
@@ -133,13 +135,13 @@
         def block(b, carry):
             block_load(*blocks[n], n, b).wait()
             block_load(*blocks[n + 1], n + 1, b).wait()
-            for j in range(width // 128):
-                at = slice(j * 128, (j + 1) * 128)
+            for start in range(0, width, 256):
+                at = slice(start, min(start + 256, width))
                 v = vals[pl.ds(pl.multiple_of(b * 128, 128), 128), at]
                 both = jnp.dot(split_gu, v, preferred_element_type=F32).astype(BF16)
                 codes = meta[pl.ds(pl.multiple_of(b * 64, 64), 64), at]
                 for p, plane in enumerate(planes(both[:64], both[64:], codes)):
-                    wgu[pl.ds(pl.multiple_of(b * 256 + p * 64, 64), 64), offset + j * 128 : offset + (j + 1) * 128] = plane
+                    wgu[pl.ds(pl.multiple_of(b * 256 + p * 64, 64), 64), offset + at.start : offset + at.stop] = plane
             return carry
 
         lax.fori_loop(0, 4, block, 0, unroll=True)
@@ -156,10 +158,6 @@
             wd[pl.ds(pl.multiple_of(b * 128, 128), 128), at] = dense.astype(BF16)
         return carry
 
-    expand_gu(gv, gm, 0, 0)
-    expand_gu(uv, um, width, 2)
-    loads[0].wait()
-    loads[1].wait()
 
     def copy(src, dst, chunk, stage, to):
         return pltpu.make_async_remote_copy(
@@ -199,28 +197,28 @@
     first_chunk = [chunk for step, chunk in order if step == "product"][0]
     first_hidden = [chunk for step, chunk in order if step == "hidden"][0]
 
-    def multiply(i, count):
-        rows = slice(0, count * ROWS)
+    def bring_together(i, count):
         weighted = (tok[i * ROWS : (i + count) * ROWS, :].astype(F32) * gain[...]).astype(BF16)
         for b in range(features // 256):
             at = slice(b * 256, (b + 1) * 256)
-            xp[rows, at] = jnp.dot(weighted[:, at], mix_x, preferred_element_type=F32).astype(BF16)
-        for n in range(2 * width // 256):
-            at = slice(n * 256, (n + 1) * 256)
-            sums = jnp.dot(xp[rows, :], wgu[:, at], preferred_element_type=F32).astype(BF16)
-            part[i : i + count, :, :, :, at] = sums.reshape(count, 2, 4, PIECE, 256)
+            xp[0 : count * ROWS, at] = jnp.dot(weighted[:, at], mix_x, preferred_element_type=F32).astype(BF16)
+
+    def multiply(i, count, first, last):
+        for start in range(first, last, 256):
+            at = slice(start, min(start + 256, last))
+            sums = jnp.dot(xp[0 : count * ROWS, :], wgu[:, at], preferred_element_type=F32).astype(BF16)
+            part[i : i + count, :, :, :, at] = sums.reshape(count, 2, 4, PIECE, at.stop - at.start)
 
     def to_partner(i):
         copy(part.at[i, 1 - c], pair_in.at[i], i, PAIR_IN, partner).start()
 
     def product(i):
         if i == first_chunk:
-            multiply(i, 1)
-            pl.semaphore_wait(barrier, len(peers))
-            to_partner(i)
-            multiply(i + 1, 1)
+            bring_together(i + 1, 1)
+            multiply(i + 1, 1, 0, 2 * width)
         else:
-            multiply(i, 2)
+            bring_together(i, 2)
+            multiply(i, 2, 0, 2 * width)
             to_partner(i)
         to_partner(i + 1)
 
@@ -230,13 +228,37 @@
     def paired(i, n, w):
         return part[i, c, n, :, sums_of(w)].astype(F32) + pair_in[i, n, :, sums_of(w)].astype(F32)
 
+    def z_first_of(i, w):
+        p1, _, other = z_of(w)
+        s1[i, w, 0] = paired(i, p1, w).astype(BF16)
+        s1[i, w, 1] = paired(i, other, w).astype(BF16)
+        copy(s1.at[i, w], z1_in.at[i, w], i, Z_FIRST, to_z(p1)).start()
+
     def z_first(i):
-        arrive(pair_in.at[i], i, PAIR_IN)
-        for w in range(2):
-            p1, _, other = z_of(w)
-            s1[i, w, 0] = paired(i, p1, w).astype(BF16)
-            s1[i, w, 1] = paired(i, other, w).astype(BF16)
-            copy(s1.at[i, w], z1_in.at[i, w], i, Z_FIRST, to_z(p1)).start()
+        if i == first_chunk:
+            arrive(pair_in.at[i, :, :, sums_of(1)], i, PAIR_UP)
+            z_first_of(i, 1)
+        else:
+            arrive(pair_in.at[i], i, PAIR_IN)
+            z_first_of(i, 0)
+            z_first_of(i, 1)
+
+    def half_to_partner(i, w, stage):
+        copy(part.at[i, 1 - c, :, :, sums_of(w)], pair_in.at[i, :, :, sums_of(w)], i, stage, partner).start()
+
+    def begin(i):
+        expand_gu(gv, gm, 0, 0)
+        loads[0].wait()
+        loads[1].wait()
+        bring_together(i, 1)
+        multiply(i, 1, 0, width)
+        pl.semaphore_wait(barrier, len(peers))
+        half_to_partner(i, 0, PAIR_GATE)
+        expand_gu(uv, um, width, 2)
+        arrive(pair_in.at[i, :, :, sums_of(0)], i, PAIR_GATE)
+        z_first_of(i, 0)
+        multiply(i, 1, width, 2 * width)
+        half_to_partner(i, 1, PAIR_UP)
 
     def z_second(i):
         arrive(z1_in.at[i], i, Z_FIRST)
@@ -292,7 +314,7 @@
             sums = jnp.dot(hid[i].reshape(ROWS, width), wd[:, at], preferred_element_type=F32).astype(BF16)
             dpart[i, :, :, :, at] = sums.reshape(2, 4, PIECE, 256)
         for v in range(2):
-            for d in range(1, 4):
+            for d in FAR_FIRST:
                 src = dpart.at[i, v, (first_of(v) + d) % 4]
                 copy(src, f_in.at[i, v, d - 1], i, F_OUT, first_peer(v, d)).start()
 
@@ -305,7 +327,7 @@
             total = total.astype(BF16)
             for q in range(4):
                 s4[i, v, q] = total[:, q * 256 : (q + 1) * 256]
-            for d in range(1, 4):
+            for d in FAR_FIRST:
                 src = s4.at[i, v, (second_of(v) + d) % 4]
                 copy(src, s_in.at[i, v, d - 1], i, S_OUT, second_peer(v, d)).start()
 
@@ -330,14 +352,14 @@
             result = own + (s5[i, v].astype(F32) + t_in[i, v].astype(F32))
             out[i, v, first_of(v), :, columns] = result.astype(BF16)
             mine = block_of(i, v, second_of(v))
-            for d in range(1, 4):
+            for d in FAR_FIRST:
                 copy(mine, mine, i, S_BACK, second_peer(v, d)).start()
 
     def f_back(i):
         arrive(s_in.at[i], i, S_BACK)
         for v in range(2):
             mine = out.at[i, v, first_of(v)]
-            for d in range(1, 4):
+            for d in FAR_FIRST:
                 copy(mine, mine, i, F_BACK, first_peer(v, d)).start()
 
     def arrived(i):
@@ -347,11 +369,13 @@
         squares=squares, product=product, z_first=z_first, z_second=z_second, hidden=hidden, z_last=z_last, pair_out=pair_out,
         expand_down=expand_down, down=down, s_out=s_out, between=between, s_back=s_back, f_back=f_back, arrive=arrived,
     )
+    begin(first_chunk)
     for step, chunk in order:
         bodies[step](chunk)
 
     for stage, whole in (
-        (PAIR_IN, pair_in), (Z_FIRST, z1_in), (Z_SECOND, z2_in), (Z_BACK, hid.at[:, 0, 0]), (Z_LAST, hid.at[:, 0, 0:2]),
+        (PAIR_GATE, pair_in.at[0, :, :, sums_of(0)]), (PAIR_UP, pair_in.at[0, :, :, sums_of(1)]), (PAIR_IN, pair_in.at[1:]),
+        (Z_FIRST, z1_in), (Z_SECOND, z2_in), (Z_BACK, hid.at[:, 0, 0]), (Z_LAST, hid.at[:, 0, 0:2]),
         (PAIR_OUT, hid.at[:, 0]), (F_OUT, f_in), (S_OUT, s_in), (BETWEEN, t_in), (S_BACK, s_in), (F_BACK, f_in),
     ):
         copy(whole, whole, 0, stage, partner).wait_send()

time: 86 us -> 86.2 us (level)
  no operation moved by 1% of the time
where the time goes in v5:
time: 86.2 us; the launch traced here: 85.1 us
  Pallas kernels  83.8 us (97%)
  local copies, waits for them, and re-layouts  1.32 us (2%)
    pallas_call x1, Pallas kernels, per_device(): pl.pallas_call(kernel, out_shape=pltpu.VMEM((CHUNKS, 2, 4, PIECE, feature...  83.8 us

profile of v5, /device:TPU:8, one launch (start us, length us, event | category | flops | bytes accessed | tf_op | source)
XLA Modules:
  0.0 85.1 jit_solution(16590176433991636073)
XLA Ops:
  0.0 83.8 %shard_map.82 = bf16[8,2,4,16,1024]{4,3,2,1,0:T(8,128)(2,1)S(1)} custom-call(bf16[1024,1024]{1,0:T(8,128)(2,1)} %tok_h.1, f32[1,1024]{1,0:T(1,128)} %bitcast.3, bf16[512,896]{1,0:T(8,128)(2,1)} %gv_h.1, s32[256,896]{1,0:T(8,128)} %gm_h.1, bf16[512,896]{1,0:T(8,128)(2,1)} %uv_h.1, s32[256,896]{1,0:T(8,128)} %um_h.1, bf16[448,1024]{1,0:T(8,128)(2,1)} %dv_h.1, ...), custom_call_target="tpu_custom_call" | custom-call | tf_op jit(solution)/shard_map/pallas_call | solution.py:407
  83.8 1.3 %copy.10 = bf16[1024,1024]{1,0:T(8,128)(2,1)} copy(bf16[1024,1024]{1,0:T(8,128)(2,1)S(1)} %bitcast.2) | data formatting | bytes 4194304
